TPU v7x, 256 devices: a whole 4x4x8 slice. The times are simulated.
256 devices in a mesh: grp: 16 (over x, z_lo, core), dev: 16 (over z_hi, y).
Axes of the slice: x: 4, y: 4, z: 8 (z_hi: 4, z_lo: 2; z = z_hi * 2 + z_lo), core: 2. Of those that a mesh axis runs over, the one named last changes fastest.
Arguments:
- a_tiles: float32 [8192, 3, 128, 128], P(('grp', 'dev')), may hold values from -1.7071068 to 18.707107
- prolong: float32 [8192, 2, 128, 128], P(('grp', 'dev')), may hold values from -0.5 to 0.5
- coarse_ids: int32 [8192, 2], P(('grp', 'dev')), may hold values from 0 to 3, as said below
Outputs:
- coarse: float32 [8192, 1536], P(('grp', 'dev'))
Inputs may be any that keep to these rules, and one draw needn't show every extreme that they name: `coarse_ids`: each fine block names 2 different coarse tiles, numbered within its own group.
All inputs are finite; a program needn't handle non-finite values.
Results may differ from a plain program's by a relative error of at most 0.0001.
Values sent between devices are 32-bit elements; how exact they have to be, the bound alone decides.
A program may use at most 128 MiB of HBM per device.

v0:
```python
import jax
import jax.numpy as jnp
from jax import lax
from jax.sharding import Mesh
from jax.sharding import PartitionSpec as P

COARSE_DEV = 32
DEV = ("dev_0", "dev_1")
GRP = ("grp_0", "grp_1", "grp_2")
GRP_DEV = ("grp_0", "grp_1", "grp_2", "dev_0", "dev_1")


def with_halo(x, sides, width):
    edges = {}
    for axis, dim in sides:
        peers, length = (lax.axis_size(axis), x.shape[dim])
        up = [(i, (i + 1) % peers) for i in range(peers)]
        last = lax.slice_in_dim(x, length - width, length, axis=dim)
        first = lax.slice_in_dim(x, 0, width, axis=dim)
        edges[dim] = (
            lax.ppermute(last, axis, up),
            lax.ppermute(first, axis, [(b, a) for a, b in up]),
        )
    done = []
    for _, dim in sides:
        low, high = edges[dim]
        around = [(width, width) if d in done else (0, 0) for d in range(x.ndim)]
        x = jnp.concatenate([jnp.pad(low, around), x, jnp.pad(high, around)], axis=dim)
        done.append(dim)
    return x


def by_axis(x, axes):
    for axis in axes:
        x = lax.psum(x, axis)
    return x


def cut_along(x, dim, peers):
    dims = x.shape
    pieces = x.reshape(*dims[:dim], peers, dims[dim] // peers, *dims[dim + 1 :])
    return jnp.moveaxis(pieces, dim, 0)


def sum_at_owner(x, axis, dim):
    peers = lax.axis_size(axis)
    pieces = lax.all_to_all(cut_along(x, dim, peers), axis, 0, 0, tiled=True)
    return jnp.sum(pieces, axis=0)


def coarse_tiles(own_a, nearby):
    block_count = own_a.shape[0]
    slot_count = nearby.shape[1]
    tile_size = nearby.shape[2]
    widened = jnp.transpose(nearby, (0, 2, 1, 3)).reshape(
        block_count + 2, tile_size, slot_count * tile_size
    )
    stacked = jnp.stack([widened[:-2], widened[1:-1], widened[2:]], axis=1)
    right_prod = jnp.einsum("bnij,bnjk->bnik", own_a, stacked, precision=lax.Precision.HIGHEST)
    right_prod = jnp.transpose(right_prod, (0, 2, 1, 3)).reshape(
        block_count, tile_size, 3 * slot_count * tile_size
    )
    left_prod = jnp.einsum(
        "bik,bic->bkc", widened[1:-1], right_prod, precision=lax.Precision.HIGHEST
    )
    left_prod = left_prod.reshape(block_count, slot_count, tile_size, 3 * slot_count, tile_size)
    return jnp.transpose(left_prod, (0, 1, 3, 2, 4))


def local(a_tiles, prolong, coarse_ids):
    fine_count = a_tiles.shape[0]
    tile_size = a_tiles.shape[-1]
    dev_count = lax.axis_size(DEV)
    grp_count = lax.axis_size(GRP)
    dev_index = lax.axis_index(DEV)
    coarse_grp = COARSE_DEV * dev_count
    ctiles = coarse_grp // tile_size
    nearby, nearby_ids = (
        with_halo(prolong, ((GRP_DEV, 0),), 1),
        with_halo(coarse_ids, ((GRP_DEV, 0),), 1),
    )
    position = jnp.arange(fine_count, dtype=jnp.int32)
    lower_win = jnp.where((position == 0) & (dev_index == 0), 0, 1).astype(jnp.int32)
    upper_win = jnp.where((position == fine_count - 1) & (dev_index == dev_count - 1), 2, 1).astype(
        jnp.int32
    )
    col_tiles = jnp.concatenate(
        [
            lower_win[:, None] * ctiles + nearby_ids[:-2],
            ctiles + coarse_ids,
            upper_win[:, None] * ctiles + nearby_ids[2:],
        ],
        axis=1,
    )
    products = coarse_tiles(a_tiles, nearby)
    partial_value = jnp.zeros((ctiles, 3 * ctiles, tile_size, tile_size), jnp.float32)
    partial_value = partial_value.at[coarse_ids[:, :, None], col_tiles[:, None, :]].add(products)
    partial_rows = jnp.transpose(partial_value, (0, 2, 1, 3)).reshape(coarse_grp, 3 * coarse_grp)
    own_trace = jnp.sum(jnp.diagonal(partial_rows[:, coarse_grp : 2 * coarse_grp]))
    trace_sum = by_axis(own_trace, GRP_DEV)
    middle_rows = sum_at_owner(partial_rows[:, coarse_grp : 2 * coarse_grp], DEV, 0)
    at_first = dev_index == 0
    at_last = dev_index == dev_count - 1
    edge_block = jnp.where(
        at_first,
        partial_rows[:, :coarse_grp],
        jnp.where(at_last, partial_rows[:, 2 * coarse_grp :], 0.0),
    )
    received = lax.all_to_all(edge_block, DEV, split_axis=0, concat_axis=0, tiled=True)
    lower_rows = received[:COARSE_DEV]
    upper_rows = received[(dev_count - 1) * COARSE_DEV :]
    owned_rows = jnp.concatenate([lower_rows, middle_rows, upper_rows], axis=1)
    mean_diag = trace_sum / (grp_count * coarse_grp)
    return owned_rows / mean_diag


def solution(mesh):
    torus = Mesh(mesh.devices.reshape(4, 2, 2, 4, 4), ("grp_0", "grp_1", "grp_2", "dev_0", "dev_1"))
    return jax.shard_map(
        local,
        mesh=torus,
        in_specs=(P(GRP_DEV, None, None, None), P(GRP_DEV, None, None, None), P(GRP_DEV, None)),
        out_specs=P(GRP_DEV, None),
        check_vma=False,
    )
```

profile of v0, /device:TPU:2, one launch (start us, length us, event | category | flops | bytes accessed | tf_op | source)
XLA Modules:
  0.0 306.3 jit_solution(531776822477899482)
XLA Ops:
  0.0 0.8 fusion.13
  0.8 1.6 collective-permute-start
  2.4 6.1 %collective-permute-start.1 = (s32[1,2]{0,1:T(2,128)S(1)}, s32[1,2]{0,1:T(2,128)S(1)}, u32[]{:S(2)}, u32[]{:S(2)}) collective-permute-start(s32[1,2]{0,1:T(2,128)S(1)} %get-tuple-element.19), channel_id=1, source_target_pairs={{1,0},{2,1},{3,2},{4,3},{5,4},{6,5},{7,6},{8,7},{9,8},{10,9},{11,1... | collective-permute-start | bytes 32 | tf_op jit(solution)/shard_map/ppermute | solution.py:22
  8.5 1.0 fusion.11
  9.5 0.1 collective-permute-start.2
  9.6 6.0 %collective-permute-start.3 = (f32[1,2,128,128]{3,2,1,0:T(8,128)S(1)}, f32[1,2,128,128]{3,2,1,0:T(8,128)S(1)}, u32[]{:S(2)}, u32[]{:S(2)}) collective-permute-start(f32[1,2,128,128]{3,2,1,0:T(8,128)S(1)} %get-tuple-element.9), channel_id=1, source_target_pairs={{1,0},{2,1},{3,2},{4,3},{5,4},{6,5},{7,6},{8,7},{9,8},{10,9},{11,1... | collective-permute-start | bytes 393224 | tf_op jit(solution)/shard_map/ppermute | solution.py:22
  15.6 0.7 clamp_shift-left_fusion.1
  16.3 0.7 clamp_compare_fusion.1
  17.0 0.1 copy.29
  17.1 0.1 copy.27
  17.2 0.0 collective-permute-done
  17.2 0.0 collective-permute-done.1
  17.2 0.8 pad_add_fusion
  18.0 0.1 slice_add_fusion
  18.1 0.1 copy.30
  18.2 0.1 copy.28
  18.3 0.1 or_select_fusion
  18.5 0.1 reshape.75
  18.6 2.3 collective-permute-done.2
  20.9 0.7 collective-permute-done.3
  21.7 2.5 maximum_bitcast_fusion
  24.2 4.7 %fusion.10 = (f32[32,128,2,128]{3,1,2,0:T(8,128)}, f32[32,128,2,128]{3,1,2,0:T(8,128)}, f32[32,128,2,128]{3,1,2,0:T(8,128)}) fusion(f32[34,128,2,128]{3,1,2,0:T(8,128)S(1)} %maximum_bitcast_fusion), kind=kLoop, calls=%fused_computation.33 | loop fusion | bytes 25165824 | tf_op jit(solution)/shard_map/slice | solution.py:58
  28.9 5.6 %copy.31 = f32[32,128,2,128]{1,3,2,0:T(8,128)} copy(f32[32,128,2,128]{3,1,2,0:T(8,128)} %get-tuple-element.7) | data formatting | bytes 8388608 | tf_op jit(solution)/shard_map/slice | solution.py:64
  34.5 5.6 %copy.32 = f32[32,128,2,128]{1,3,2,0:T(8,128)} copy(f32[32,128,2,128]{3,1,2,0:T(8,128)} %get-tuple-element.5) | data formatting | bytes 8388608 | tf_op jit(solution)/shard_map/slice | solution.py:58
  40.1 5.6 %copy.34 = f32[32,128,2,128]{1,3,2,0:T(8,128)} copy(f32[32,128,2,128]{3,1,2,0:T(8,128)} %get-tuple-element.6) | data formatting | bytes 8388608 | tf_op jit(solution)/shard_map/slice | solution.py:58
  45.7 15.3 %fusion = f32[32,3,256,128]{3,2,1,0:T(8,128)S(1)} fusion(f32[32,3,128,128]{3,2,1,0:T(8,128)} %param.3, f32[32,1,128,256]{2,3,1,0:T(8,128)} %bitcast.41, f32[32,1,128,256]{2,3,1,0:T(8,128)} %bitcast.37, f32[32,1,128,256]{2,3,1,0:T(8,128)} %bitcast.40), kind=kOutput, calls=%fused_computation.2 | convolution fusion | flops 4838129664 | bytes 31457280 | tf_op jit(solution)/shard_map/bnij,bnjk->bnik/dot_general | solution.py:59
  61.1 23.4 %fusion.14 = f32[32,256,768]{1,2,0:T(8,128)} fusion(f32[32,128,256]{1,2,0:T(8,128)S(1)} %bitcast.38, f32[32,128,768]{1,2,0:T(8,128)S(1)} %bitcast.35), kind=kOutput, calls=%fused_computation.37 | convolution fusion | flops 9663676416 | bytes 41943040 | tf_op jit(solution)/shard_map/bik,bic->bkc/dot_general | solution.py:63
  84.5 30.8 %reshape.66 = f32[32,2,128,6,128]{2,1,4,3,0:T(2,128)} reshape(f32[32,256,768]{1,2,0:T(8,128)} %fusion.14) | data formatting | bytes 50331648 | tf_op jit(solution)/shard_map/reshape | solution.py:66
  115.2 36.9 %copy.37 = f32[32,2,6,128,128]{4,3,2,1,0:T(8,128)} copy(f32[32,2,6,128,128]{3,1,4,2,0:T(2,128)} %bitcast.36) | data formatting | bytes 50331648 | tf_op jit(solution)/shard_map/transpose | solution.py:67
  152.1 0.4 broadcast_in_dim.35
  152.5 52.5 %scatter_fusion = f32[4,12,128,128]{3,2,1,0:T(8,128)S(1)} fusion(f32[4,12,128,128]{3,2,1,0:T(8,128)S(1)} %broadcast_in_dim.35, s32[384]{0:T(512)S(1)} %reshape.75, f32[384,128,128]{2,1,0:T(8,128)} %bitcast.34), kind=kCustom, calls=%fused_computation.1 | custom fusion | flops 6291456 | bytes 75500544 | tf_op jit(solution)/shard_map/scatter-add | solution.py:97
  205.0 2.8 copy.38
  207.8 2.2 copy.46
  210.0 0.3 fusion.12
  210.4 1.3 copy.39
  211.7 8.6 %all-to-all-start = ((f32[16,32,512]{2,1,0:T(8,128)}), f32[16,32,512]{2,1,0:T(8,128)S(1)}, u32[]{:S(2)}, u32[]{:S(2)}) async-start(f32[16,32,512]{2,1,0:T(8,128)} %bitcast.10), calls=%async_computation | async-start | bytes 2097152 | tf_op jit(solution)/shard_map/all_to_all | solution.py:109
  220.3 1.4 copy.43
  221.7 20.8 %all-to-all-done = f32[16,32,512]{2,1,0:T(8,128)S(1)} async-done(((f32[16,32,512]{2,1,0:T(8,128)}), f32[16,32,512]{2,1,0:T(8,128)S(1)}, u32[]{:S(2)}, u32[]{:S(2)}) %all-to-all-start) | async-done | bytes 1048608 | tf_op jit(solution)/shard_map/all_to_all | solution.py:109
  242.5 9.9 %all-to-all-start.1 = ((f32[16,32,512]{2,1,0:T(8,128)}), f32[16,32,512]{2,1,0:T(8,128)S(1)}, u32[]{:S(2)}, u32[]{:S(2)}) async-start(f32[16,32,512]{2,1,0:T(8,128)} %bitcast.12), calls=%async_computation.1 | async-start | bytes 2097152 | tf_op jit(solution)/shard_map/all_to_all | solution.py:47
  252.4 8.5 %gather_fusion = f32[512]{0:T(512)S(1)} fusion(f32[512,512]{1,0:T(8,128)} %copy.43, s32[512]{0:T(512)S(1)} %bitcast.39), kind=kCustom, calls=%fused_computation | custom fusion | bytes 8192 | tf_op jit(solution)/shard_map/jit(diagonal)/cond/branch_0_fun/gather | solution.py:99
  260.9 0.6 reduce_sum.19
  261.5 9.5 %psum.35 = f32[]{:T(128)} all-reduce(f32[]{:T(128)} %reduce_sum.19), channel_id=1, replica_groups=mesh['grp_0'=4,'grp_1'=2,'grp_2'=2,'dev_0'=4,'dev_1'=4] {'grp_0'}, use_global_device_ids=true, to_apply=%region_3.4 | all-reduce | flops 1 | bytes 8 | tf_op jit(solution)/shard_map/psum | solution.py:35
  270.9 6.5 %psum.36 = f32[]{:T(128)} all-reduce(f32[]{:T(128)} %psum.35), channel_id=1, replica_groups=mesh['grp_0'=4,'grp_1'=2,'grp_2'=2,'dev_0'=4,'dev_1'=4] {'grp_1'}, use_global_device_ids=true, to_apply=%region_4.5 | all-reduce | flops 1 | bytes 8 | tf_op jit(solution)/shard_map/psum | solution.py:35
  277.4 3.1 %psum.37 = f32[]{:T(128)} all-reduce(f32[]{:T(128)} %psum.36), channel_id=1, replica_groups=mesh['grp_0'=4,'grp_1'=2,'grp_2'=2,'dev_0'=4,'dev_1'=4] {'grp_2'}, use_global_device_ids=true, to_apply=%region_5.6 | all-reduce | flops 1 | bytes 8 | tf_op jit(solution)/shard_map/psum | solution.py:35
  280.5 13.3 %psum.38 = f32[]{:T(128)} all-reduce(f32[]{:T(128)} %psum.37), channel_id=1, replica_groups=mesh['grp_0'=4,'grp_1'=2,'grp_2'=2,'dev_0'=4,'dev_1'=4] {'dev_0'}, use_global_device_ids=true, to_apply=%region_6.7 | all-reduce | flops 1 | bytes 8 | tf_op jit(solution)/shard_map/psum | solution.py:35
  293.8 11.0 %psum.39 = f32[]{:T(128)} all-reduce(f32[]{:T(128)} %psum.38), channel_id=1, replica_groups=mesh['grp_0'=4,'grp_1'=2,'grp_2'=2,'dev_0'=4,'dev_1'=4] {'dev_1'}, use_global_device_ids=true, to_apply=%region_7.8 | all-reduce | flops 1 | bytes 8 | tf_op jit(solution)/shard_map/psum | solution.py:35
  305.5 0.1 reduce_sum.18
  305.6 0.7 maximum_divide_fusion
  (9 shorter events, 0.1 us)
Async XLA Ops:
  0.8 16.4 %collective-permute-start = (s32[1,2]{0,1:T(2,128)S(1)}, s32[1,2]{0,1:T(2,128)S(1)}, u32[]{:S(2)}, u32[]{:S(2)}) collective-permute-start(s32[1,2]{0,1:T(2,128)S(1)} %get-tuple-element.18), channel_id=1, source_target_pairs={{0,1},{1,2},{2,3},{3,4},{4,5},{5,6},{6,7},{7,8},{8,9},{9,10},{10,1... | collective-permute-start | bytes 32 | tf_op jit(solution)/shard_map/ppermute | solution.py:21
  2.4 14.8 %collective-permute-start.1 = (s32[1,2]{0,1:T(2,128)S(1)}, s32[1,2]{0,1:T(2,128)S(1)}, u32[]{:S(2)}, u32[]{:S(2)}) collective-permute-start(s32[1,2]{0,1:T(2,128)S(1)} %get-tuple-element.19), channel_id=1, source_target_pairs={{1,0},{2,1},{3,2},{4,3},{5,4},{6,5},{7,6},{8,7},{9,8},{10,9},{11,1... | collective-permute-start | bytes 32 | tf_op jit(solution)/shard_map/ppermute | solution.py:22
  9.5 11.4 %collective-permute-start.2 = (f32[1,2,128,128]{3,2,1,0:T(8,128)S(1)}, f32[1,2,128,128]{3,2,1,0:T(8,128)S(1)}, u32[]{:S(2)}, u32[]{:S(2)}) collective-permute-start(f32[1,2,128,128]{3,2,1,0:T(8,128)S(1)} %get-tuple-element.8), channel_id=1, source_target_pairs={{0,1},{1,2},{2,3},{3,4},{4,5},{5,6},{6,7},{7,8},{8,9},{9,10},{10,1... | collective-permute-start | bytes 393224 | tf_op jit(solution)/shard_map/ppermute | solution.py:21
  9.6 12.0 %collective-permute-start.3 = (f32[1,2,128,128]{3,2,1,0:T(8,128)S(1)}, f32[1,2,128,128]{3,2,1,0:T(8,128)S(1)}, u32[]{:S(2)}, u32[]{:S(2)}) collective-permute-start(f32[1,2,128,128]{3,2,1,0:T(8,128)S(1)} %get-tuple-element.9), channel_id=1, source_target_pairs={{1,0},{2,1},{3,2},{4,3},{5,4},{6,5},{7,6},{8,7},{9,8},{10,9},{11,1... | collective-permute-start | bytes 393224 | tf_op jit(solution)/shard_map/ppermute | solution.py:22
  45.7 15.3 %copy-start = (f32[32,128,2,128]{1,3,2,0:T(8,128)S(1)}, f32[32,128,2,128]{1,3,2,0:T(8,128)}, u32[]{:S(2)}) copy-start(f32[32,128,2,128]{1,3,2,0:T(8,128)} %copy.31) | copy-start | bytes 12582916
  211.7 30.8 %all-to-all-start = ((f32[16,32,512]{2,1,0:T(8,128)}), f32[16,32,512]{2,1,0:T(8,128)S(1)}, u32[]{:S(2)}, u32[]{:S(2)}) async-start(f32[16,32,512]{2,1,0:T(8,128)} %bitcast.10), calls=%async_computation | async-start | bytes 2097152 | tf_op jit(solution)/shard_map/all_to_all | solution.py:109
  242.5 63.0 %all-to-all-start.1 = ((f32[16,32,512]{2,1,0:T(8,128)}), f32[16,32,512]{2,1,0:T(8,128)S(1)}, u32[]{:S(2)}, u32[]{:S(2)}) async-start(f32[16,32,512]{2,1,0:T(8,128)} %bitcast.12), calls=%async_computation.1 | async-start | bytes 2097152 | tf_op jit(solution)/shard_map/all_to_all | solution.py:47
where the time goes:
time: 311 us; the launch traced here: 306 us
  local copies, waits for them, and re-layouts  108 us (35%)
  other arithmetic  59.2 us (19%)
  blocking collectives  43.3 us (14%)
  matrix products  38.7 us (12%)
  starting transfers between devices  32.3 us (10%)
  waiting for transfers between devices  23.8 us (8%)
    scatter-add x1, other arithmetic, local(): partial_value.at[coarse_ids[:, :, None], col_tiles[:, None, :]]  52.5 us
    psum x5, blocking collectives, by_axis(): x = lax.psum(x, axis)  43.3 us
    transpose x1, local copies, waits for them, and re-layouts, coarse_tiles(): return jnp.transpose(left_prod, (0, 1, 3, 2, 4))  36.9 us
    reshape x1, local copies, waits for them, and re-layouts, coarse_tiles(): left_prod.reshape(block_count, slot_count, tile_size, 3 * slot_count, til...  30.8 us
    dot_general x1, matrix products, coarse_tiles(): jnp.einsum('bik,bic->bkc', widened[1:-1], right_prod, precision=lax.Preci...  23.4 us
    all_to_all x1, waiting for transfers between devices, local(): lax.all_to_all(edge_block, DEV, split_axis=0, concat_axis=0, tiled=True)  20.8 us
    slice x3, local copies, waits for them, and re-layouts, coarse_tiles(): stacked = jnp.stack([widened[:-2], widened[1:-1], widened[2:]], axis=1)  16 us
    dot_general x1, matrix products, coarse_tiles(): jnp.einsum('bnij,bnjk->bnik', own_a, stacked, precision=lax.Precision.HIG...  15.3 us
  transfers between devices with their start and end apart: 6, of which 3 were waited for; matrix products, arithmetic and copies ran while one was open for 5% of the time, Pallas kernels for 0%

commit v1 on v0

v1 whole, which is shorter than its diff:
```python
import jax
import jax.numpy as jnp
from jax import lax
from jax.experimental import pallas as pl
from jax.experimental.pallas import tpu as pltpu
from jax.sharding import Mesh
from jax.sharding import PartitionSpec as P

GRP_DEV = ("grp_0", "grp_1", "grp_2", "dev_0", "dev_1")
AXES = GRP_DEV
NB = 32
T = 128
CT = 4
PZ = 192
F32 = jnp.float32
BF16 = jnp.bfloat16


def coords(index):
    grp, dev = index // 16, index % 16
    return (grp // 4, grp // 2 % 2, grp % 2, dev // 4, dev % 4)


def split(x):
    hi = x.astype(BF16)
    lo = (x - hi.astype(F32)).astype(BF16)
    return hi, lo


def twice(x):
    return jnp.concatenate([x, x], axis=1)


def kernel(
    ids,
    a_hbm,
    p_hbm,
    out,
    a_buf,
    p_buf,
    pt,
    prod,
    r2,
    halo,
    halo_id,
    id_send,
    c_send,
    y_a,
    y_b,
    y_d,
    z_send,
    z_recv,
    e_send,
    e_recv,
    t_send,
    t_one,
    t_two,
    sem_a,
    sem_p,
    sem_hs,
    sem_hr,
    sem_ys,
    sem_yr,
    sem_zs,
    sem_zr,
    sem_es,
    sem_er,
    sem_ts,
    sem_tr,
):
    gx, gz, gc, dz, dy = (lax.axis_index(name) for name in AXES)
    grp = gx * 4 + gz * 2 + gc
    dev = dz * 4 + dy
    me = grp * 16 + dev

    def dev_peer(rel):
        other = lax.rem(dev + rel, 16)
        return (gx, gz, gc, other // 4, lax.rem(other, 4))

    def grp_peer(rel):
        other = lax.rem(grp + rel, 16)
        return (other // 4, lax.rem(other // 2, 2), lax.rem(other, 2), dz, dy)

    def y_peer(rel):
        return (gx, gz, gc, dz, lax.rem(dy + rel, 4))

    def z_peer(rel):
        return (gx, gz, gc, lax.rem(dz + rel, 4), dy)

    def ring_peer(rel):
        other = lax.rem(me + rel, 256)
        g, d = other // 16, lax.rem(other, 16)
        return (g // 4, lax.rem(g // 2, 2), lax.rem(g, 2), d // 4, lax.rem(d, 4))

    nxt, prv = ring_peer(1), ring_peer(255)
    barrier = pltpu.get_barrier_semaphore()
    for peer in [nxt, prv] + [dev_peer(k) for k in range(1, 16)] + [grp_peer(k) for k in range(1, 16)]:
        pl.semaphore_signal(barrier, inc=1, device_id=peer, device_id_type=pl.DeviceIdType.MESH)

    def remote(src, dst, send, recv, peer):
        return pltpu.make_async_remote_copy(
            src_ref=src,
            dst_ref=dst,
            send_sem=send,
            recv_sem=recv,
            device_id=peer,
            device_id_type=pl.DeviceIdType.MESH,
        )

    def load_a(g):
        cut = pl.ds(g * 4, 4)
        return pltpu.make_async_copy(a_hbm.at[cut], a_buf.at[cut], sem_a.at[g])

    def load_p(g):
        cut = pl.ds(g * 4, 4)
        return pltpu.make_async_copy(p_hbm.at[cut], p_buf.at[cut], sem_p.at[g])

    load_p(0).start()
    load_a(0).start()
    load_a(1).start()
    load_p(7).start()
    for g in range(1, 7):
        load_p(g).start()
        load_a(g + 1).start()

    zero_f = jnp.zeros((T, T), F32)
    zero_b = jnp.zeros((T, T), BF16)
    prod[PZ] = zero_f
    pt[64] = zero_b
    pt[129] = zero_b
    for side, block in ((0, 0), (1, NB - 1)):
        for slot in range(2):
            id_send[side, :, slot * T : (slot + 1) * T] = jnp.full((8, T), ids[block, slot], jnp.int32)

    def pick(block, j, first, none):
        return jnp.where(ids[block, 0] == j, first, jnp.where(ids[block, 1] == j, first + 1, none))

    def push_p(p0, p1, unit):
        h0, l0 = split(p0)
        h1, l1 = split(p1)
        high, low = jnp.concatenate([h0, h1], axis=1), jnp.concatenate([l0, l1], axis=1)
        pltpu.matmul_push_rhs(jnp.concatenate([high, low], axis=0), 0, unit)
        return (h0, h1), (l0, l1)

    def gather(n0, n1, n2, j, ends):
        total = prod[pick(n1, j, n1 * 6 + 2, PZ)]
        if ends != 0:
            total = total + prod[pick(n0, j, n0 * 6, PZ)]
        if ends != 1:
            total = total + prod[pick(n2, j, n2 * 6 + 4, PZ)]
        return total

    def put_r(pair, half, j, value):
        hi, lo = split(value)
        r2[pair, 0, half * T : (half + 1) * T, j * T : (j + 1) * T] = hi
        r2[pair, 1, half * T : (half + 1) * T, j * T : (j + 1) * T] = lo

    def assemble(pair):
        for half in range(2):
            block = pair * 2 - 1 + half
            low = jnp.maximum(block - 1, 0)
            mid = jnp.maximum(block, 0)
            for j in range(CT):
                put_r(pair, half, j, gather(low, mid, block + 1, j, None))

    def body(acc0, acc1, tot):
        acc = (acc0, acc1)

        def products(t):
            for unit in range(2):
                n = t * 2 + unit
                high, low = push_p(p_buf[n, 0], p_buf[n, 1], unit)
                for slot in range(2):
                    pt[n * 2 + slot] = high[slot].T
                    pt[65 + n * 2 + slot] = low[slot].T
                for m in range(3):
                    hi, lo = split(a_buf[jnp.clip(n + 1 - m, 0, NB - 1), m])
                    pltpu.matmul_acc_lhs(acc[unit][m], twice(hi), load_staged_rhs=0 if m == 0 else None)
                    pltpu.matmul_acc_lhs(acc[unit][m], twice(lo))

        def drain(t):
            for unit in range(2):
                n = t * 2 + unit
                for m in range(3):
                    res = pltpu.matmul_pop(acc[unit][m])
                    prod[(n * 3 + m) * 2] = res[:, :T]
                    prod[(n * 3 + m) * 2 + 1] = res[:, T:]

        def step(t):
            products(t)
            assemble(jnp.maximum(t - 1, 0))
            drain(t)

        def one_group(g, carry):
            load_p(g).wait()

            @pl.when(g < 7)
            def _():
                load_a(g + 1).wait()

            step(g * 2)
            step(g * 2 + 1)
            return carry

        load_p(0).wait()
        load_a(0).wait()
        load_a(1).wait()
        step(0)
        step(1)
        load_p(7).wait()

        pl.semaphore_wait(barrier, 32)
        halo_copies = [
            remote(p_buf.at[NB - 1], halo.at[0], sem_hs.at[0], sem_hr.at[0], nxt),
            remote(p_buf.at[0], halo.at[1], sem_hs.at[1], sem_hr.at[1], prv),
            remote(id_send.at[1], halo_id.at[0], sem_hs.at[2], sem_hr.at[2], nxt),
            remote(id_send.at[0], halo_id.at[1], sem_hs.at[3], sem_hr.at[3], prv),
        ]
        for copy in halo_copies:
            copy.start()

        def later_group(g, carry):
            load_p(g).wait()
            load_a(g + 1).wait()
            step(g * 2)
            step(g * 2 + 1)
            return carry

        lax.fori_loop(1, 7, later_group, 0)
        step(14)
        step(15)
        assemble(15)

        for copy in halo_copies:
            copy.wait_recv()
        for side in range(2):
            push_p(halo[side, 0], halo[side, 1], side)
            hi, lo = split(a_buf[0, 0] if side == 0 else a_buf[NB - 1, 2])
            pltpu.matmul_acc_lhs(acc[side][0], twice(hi), load_staged_rhs=0)
            pltpu.matmul_acc_lhs(acc[side][0], twice(lo))
        edge = [pltpu.matmul_pop(acc[side][0]) for side in range(2)]
        for side in range(2):
            prod[193 + side * 2] = edge[side][:, :T]
            prod[194 + side * 2] = edge[side][:, T:]
        inner = [dev > 0, dev < 15]
        for half, side in ((0, 1), (1, 0)):
            for j in range(CT):
                own = gather(30, 31, 31, j, 1) if side == 1 else gather(0, 0, 1, j, 0)
                extra = zero_f
                for slot in range(2):
                    match = halo_id[side, 0:1, slot * T : (slot + 1) * T] == j
                    extra = extra + jnp.where(match, prod[193 + side * 2 + slot], 0.0)
                put_r(0, half, j, own + jnp.where(inner[side], extra, 0.0))

        def lhs(b0, b1, i, low):
            base = 65 if low else 0
            none = 129 if low else 64
            return jnp.concatenate(
                [pt[pick(b0, i, base + b0 * 2, none)], pt[pick(b1, i, base + b1 * 2, none)]], axis=1
            )

        for side, at in ((0, 0), (1, 15)):

            @pl.when(dev == at)
            def _(side=side):
                block = 0 if side == 0 else NB - 1
                y0, y1 = prod[193 + side * 2], prod[194 + side * 2]
                h0, l0 = split(y0)
                h1, l1 = split(y1)
                for part, (q0, q1) in enumerate(((h0, h1), (l0, l1))):
                    row = jnp.concatenate([q0, q1], axis=1)
                    for unit in range(2):
                        pltpu.matmul_push_rhs(jnp.concatenate([row, row], axis=0), 0, unit)
                        left = [
                            jnp.concatenate(
                                [pt[pick(block, i, block * 2, 64)], pt[pick(block, i, 65 + block * 2, 129)]], axis=1
                            )
                            for i in (unit * 2, unit * 2 + 1)
                        ]
                        pltpu.matmul_acc_lhs(tot[unit], jnp.concatenate(left, axis=0), load_staged_rhs=0)
                for unit in range(2):
                    res = pltpu.matmul_pop(tot[unit])
                    for k in range(8):
                        e_send[side, unit * 8 + k, 0:32] = res[k * 32 : (k + 1) * 32]
                code = halo_id[side].astype(F32)
                for k in range(16):
                    e_send[side, k, 32:40] = code
                for rel in range(1, 16):
                    other = lax.rem(dev + rel, 16)
                    remote(
                        e_send.at[side, other], e_recv.at[side], sem_es.at[side, rel], sem_er.at[side], dev_peer(rel)
                    ).start()
                e_recv[side] = e_send[side, at]

        def totals(chunk):
            columns = slice(chunk * 2 * T, (chunk + 1) * 2 * T)

            def pair_step(pair, b0, b1):
                for unit in range(2):
                    rows = (unit * 2, unit * 2 + 1)
                    high = jnp.concatenate([lhs(b0, b1, i, False) for i in rows], axis=0)
                    low = jnp.concatenate([lhs(b0, b1, i, True) for i in rows], axis=0)
                    pltpu.matmul_push_rhs(r2[pair, 0, :, columns], 0, unit)
                    pltpu.matmul_push_rhs(r2[pair, 1, :, columns], 1, unit)
                    pltpu.matmul_acc_lhs(tot[unit], high, load_staged_rhs=0)
                    pltpu.matmul_acc_lhs(tot[unit], low)
                    pltpu.matmul_acc_lhs(tot[unit], high, load_staged_rhs=1)

            def three(k, carry):
                for u in range(3):
                    pair = k * 3 + 1 + u
                    pair_step(pair, pair * 2 - 1, pair * 2)
                return carry

            lax.fori_loop(0, 5, three, 0)
            pair_step(0, NB - 1, 0)
            eye = (
                lax.broadcasted_iota(jnp.int32, (T, T), 0) == lax.broadcasted_iota(jnp.int32, (T, T), 1)
            )
            diag = jnp.zeros((8, T), F32)
            for unit in range(2):
                res = pltpu.matmul_pop(tot[unit])
                for half in range(2):
                    i = unit * 2 + half
                    for y in range(4):
                        c_send[chunk, y, i] = res[half * T + y * 32 : half * T + (y + 1) * 32]
                if unit == chunk:
                    for half in range(2):
                        tile = jnp.where(eye, res[half * T : (half + 1) * T, half * T : (half + 1) * T], 0.0)
                        diag = diag + jnp.sum(tile.reshape(16, 8, T), axis=0)
            return diag

        up, down = lax.rem(dy + 1, 4), lax.rem(dy + 3, 4)
        far = lax.rem(dy + 2, 4)
        lo2, hi2 = pl.ds(0, 2), pl.ds(2, 2)

        def y_first(c):
            return [
                remote(c_send.at[c, far, lo2], y_a.at[c, 0], sem_ys.at[c, 0], sem_yr.at[c, 0], y_peer(1)),
                remote(c_send.at[c, far, hi2], y_a.at[c, 1], sem_ys.at[c, 1], sem_yr.at[c, 1], y_peer(3)),
                remote(c_send.at[c, up, hi2], y_d.at[c, 0], sem_ys.at[c, 2], sem_yr.at[c, 2], y_peer(1)),
                remote(c_send.at[c, down, lo2], y_d.at[c, 1], sem_ys.at[c, 3], sem_yr.at[c, 3], y_peer(3)),
            ]

        def y_second(c):
            return [
                remote(c_send.at[c, up, lo2], y_b.at[c, 0], sem_ys.at[c, 4], sem_yr.at[c, 4], y_peer(1)),
                remote(c_send.at[c, down, hi2], y_b.at[c, 1], sem_ys.at[c, 5], sem_yr.at[c, 5], y_peer(3)),
            ]

        def z_all(c):
            return [
                remote(
                    z_send.at[c, lax.rem(dz + rel, 4)],
                    z_recv.at[c, rel - 1],
                    sem_zs.at[c, rel - 1],
                    sem_zr.at[c, rel - 1],
                    z_peer(rel),
                )
                for rel in range(1, 4)
            ]

        def begin_second(c):
            first = y_first(c)
            first[0].wait_recv()
            c_send[c, up, lo2] = c_send[c, up, lo2] + y_a[c, 0]
            y_second(c)[0].start()
            first[1].wait_recv()
            c_send[c, down, hi2] = c_send[c, down, hi2] + y_a[c, 1]
            y_second(c)[1].start()

        def begin_z(c):
            for copy in y_first(c)[2:] + y_second(c):
                copy.wait_recv()
            z_send[c, 0:2] = c_send[c, dy, lo2] + y_b[c, 0] + y_d[c, 1]
            z_send[c, 2:4] = c_send[c, dy, hi2] + y_b[c, 1] + y_d[c, 0]
            for copy in z_all(c):
                copy.start()

        diag = totals(0)
        for copy in y_first(0):
            copy.start()
        diag = diag + totals(1)
        t_send[0] = diag

        def t_copies(phase):
            into = t_one if phase == 0 else t_two
            peer = dev_peer if phase == 0 else grp_peer
            return [
                remote(t_send.at[phase], into.at[rel], sem_ts.at[phase, rel], sem_tr.at[phase, rel], peer(rel))
                for rel in range(1, 16)
            ]

        one, two = t_copies(0), t_copies(1)
        for copy in one:
            copy.start()
        for copy in y_first(1):
            copy.start()
        begin_second(0)
        begin_second(1)
        begin_z(0)
        begin_z(1)
        total = diag
        for rel in range(1, 16):
            one[rel - 1].wait_recv()
            total = total + t_one[rel]
        t_send[1] = total
        for copy in two:
            copy.start()
        for rel in range(1, 16):
            two[rel - 1].wait_recv()
            total = total + t_two[rel]
        mean = jnp.sum(total, axis=(0, 1), keepdims=True) * (1.0 / 8192.0)
        scale = jnp.broadcast_to(mean, (32, 2 * T))

        for side, at in ((0, 0), (1, 15)):
            base = 0 if side == 0 else 1024

            @pl.when(dev != at)
            def _(side=side):
                remote(
                    e_send.at[side, 0], e_recv.at[side], sem_es.at[side, 0], sem_er.at[side], dev_peer(1)
                ).wait_recv()

            for j in range(CT):
                value = jnp.zeros((32, T), F32)
                for slot in range(2):
                    match = e_recv[side, 32:33, slot * T : (slot + 1) * T] == float(j)
                    value = value + jnp.where(match, e_recv[side, 0:32, slot * T : (slot + 1) * T], 0.0)
                out[:, base + j * T : base + (j + 1) * T] = value / scale[:, :T]

        for c in range(2):
            value = z_send[c, dz]
            for k, copy in enumerate(z_all(c)):
                copy.wait_recv()
                value = value + z_recv[c, k]
            out[:, 512 + c * 256 : 512 + (c + 1) * 256] = value / scale

        for copy in halo_copies + one + two:
            copy.wait_send()
        for c in range(2):
            for copy in y_first(c) + y_second(c) + z_all(c):
                copy.wait_send()
        for side, at in ((0, 0), (1, 15)):

            @pl.when(dev == at)
            def _(side=side):
                for rel in range(1, 16):
                    remote(
                        e_send.at[side, 0], e_recv.at[side], sem_es.at[side, rel], sem_er.at[side], dev_peer(rel)
                    ).wait_send()

    small = tuple(tuple(pltpu.ACC(unit)((T, 2 * T), F32) for _ in range(3)) for unit in range(2))
    large = tuple(pltpu.ACC(unit)((2 * T, 2 * T), F32) for unit in range(2))
    pl.run_scoped(body, small[0], small[1], large)


def local(a_tiles, prolong, coarse_ids):
    vmem, dma = pltpu.VMEM, pltpu.SemaphoreType.DMA
    return pl.pallas_call(
        kernel,
        out_shape=jax.ShapeDtypeStruct((32, 1536), F32),
        in_specs=[
            pl.BlockSpec(memory_space=pltpu.SMEM),
            pl.BlockSpec(memory_space=pl.ANY),
            pl.BlockSpec(memory_space=pl.ANY),
        ],
        out_specs=pl.BlockSpec(memory_space=pltpu.VMEM),
        scratch_shapes=[
            vmem((NB, 3, T, T), F32),
            vmem((NB, 2, T, T), F32),
            vmem((130, T, T), BF16),
            vmem((197, T, T), F32),
            vmem((16, 2, 2 * T, 4 * T), BF16),
            vmem((2, 2, T, T), F32),
            vmem((2, 8, 2 * T), jnp.int32),
            vmem((2, 8, 2 * T), jnp.int32),
            vmem((2, 4, 4, 32, 2 * T), F32),
            vmem((2, 2, 2, 32, 2 * T), F32),
            vmem((2, 2, 2, 32, 2 * T), F32),
            vmem((2, 2, 2, 32, 2 * T), F32),
            vmem((2, 4, 32, 2 * T), F32),
            vmem((2, 3, 32, 2 * T), F32),
            vmem((2, 16, 40, 2 * T), F32),
            vmem((2, 40, 2 * T), F32),
            vmem((2, 8, T), F32),
            vmem((16, 8, T), F32),
            vmem((16, 8, T), F32),
            dma((8,)),
            dma((8,)),
            dma((4,)),
            dma((4,)),
            dma((2, 6)),
            dma((2, 6)),
            dma((2, 3)),
            dma((2, 3)),
            dma((2, 16)),
            dma((2,)),
            dma((2, 16)),
            dma((2, 16)),
        ],
        compiler_params=pltpu.CompilerParams(
            collective_id=0, has_side_effects=True, vmem_limit_bytes=60 * 1024 * 1024
        ),
    )(coarse_ids, a_tiles, prolong)


def solution(mesh):
    torus = Mesh(mesh.devices.reshape(4, 2, 2, 4, 4), GRP_DEV)

    def run(a_tiles, prolong, coarse_ids):
        return jax.shard_map(
            local,
            mesh=torus,
            in_specs=(P(GRP_DEV, None, None, None), P(GRP_DEV, None, None, None), P(GRP_DEV, None)),
            out_specs=P(GRP_DEV, None),
            check_vma=False,
        )(a_tiles, prolong, coarse_ids)

    return run
```

time: 311 us -> 49.5 us (0.16)
  the two profiles are of different devices: /device:TPU:2 before, /device:TPU:1 now
where the time goes in v1:
time: 49.5 us; the launch traced here: 49.3 us
  Pallas kernels  46.3 us (94%)
  local copies, waits for them, and re-layouts  2.98 us (6%)
    pallas_call x1, Pallas kernels, local(): pl.pallas_call(kernel, out_shape=jax.ShapeDtypeStruct((32, 1536), F32), i...  46.3 us
    unnamed x2, local copies, waits for them, and re-layouts  2.98 us

profile of v1, /device:TPU:1, one launch (start us, length us, event | category | flops | bytes accessed | tf_op | source)
XLA Modules:
  0.0 49.3 jit_solution(16921654593706854066)
XLA Ops:
  0.0 1.4 %copy.4.ids = s32[32,2]{1,0:T(8,128)} copy(s32[32,2]{0,1:T(2,128)} %param.5) | data formatting | bytes 512 | tf_op args[2]
  1.4 46.3 %shard_map.37 = f32[32,1536]{1,0:T(8,128)} custom-call(s32[32,2]{1,0:T(8,128)} %copy.4.ids, f32[32,3,128,128]{3,2,1,0:T(8,128)} %a_hbm.1, f32[32,2,128,128]{3,2,1,0:T(8,128)} %p_hbm.1), custom_call_target="tpu_custom_call" | custom-call | tf_op jit(solution)/shard_map/pallas_call | solution.py:460
  47.7 1.6 %copy.6 = f32[32,1536]{1,0:T(8,128)} copy(f32[32,1536]{1,0:T(8,128)} %shard_map.37) | data formatting | bytes 393216

commit v2 on v1

v2 whole, which is shorter than its diff:
```python
import jax
import jax.numpy as jnp
from jax import lax
from jax.experimental import pallas as pl
from jax.experimental.pallas import tpu as pltpu
from jax.sharding import Mesh
from jax.sharding import PartitionSpec as P

GRP_DEV = ("grp_0", "grp_1", "grp_2", "dev_0", "dev_1")
AXES = GRP_DEV
NB = 32
T = 128
CT = 4
PZ = 192
VMEM_MIB = 53
F32 = jnp.float32
BF16 = jnp.bfloat16


def coords(index):
    grp, dev = index // 16, index % 16
    return (grp // 4, grp // 2 % 2, grp % 2, dev // 4, dev % 4)


def split(x):
    hi = x.astype(BF16)
    lo = (x - hi.astype(F32)).astype(BF16)
    return hi, lo


def rest(x):
    return x - x.astype(BF16).astype(F32)


def twice(x):
    return jnp.concatenate([x, x], axis=1)


def kernel(
    ids,
    a_hbm,
    p_hbm,
    out,
    a_buf,
    p_buf,
    pt,
    prod,
    r2,
    halo,
    halo_id,
    id_send,
    c_send,
    y_a,
    y_b,
    y_d,
    z_send,
    z_a,
    z_b,
    z_d,
    e_send,
    e_y,
    e_pass,
    e_recv,
    t_send,
    t_one,
    t_two,
    sem_a,
    sem_p,
    sem_hs,
    sem_hr,
    sem_ys,
    sem_yr,
    sem_zs,
    sem_zr,
    sem_es,
    sem_er,
    sem_ts,
    sem_tr,
):
    gx, gz, gc, dz, dy = (lax.axis_index(name) for name in AXES)
    grp = gx * 4 + gz * 2 + gc
    dev = dz * 4 + dy
    me = grp * 16 + dev

    def dev_peer(rel):
        other = lax.rem(dev + rel, 16)
        return (gx, gz, gc, other // 4, lax.rem(other, 4))

    def grp_peer(rel):
        other = lax.rem(grp + rel, 16)
        return (other // 4, lax.rem(other // 2, 2), lax.rem(other, 2), dz, dy)

    def y_peer(rel):
        return (gx, gz, gc, dz, lax.rem(dy + rel, 4))

    def z_peer(rel):
        return (gx, gz, gc, lax.rem(dz + rel, 4), dy)

    def ring_peer(rel):
        other = lax.rem(me + rel, 256)
        g, d = other // 16, lax.rem(other, 16)
        return (g // 4, lax.rem(g // 2, 2), lax.rem(g, 2), d // 4, lax.rem(d, 4))

    def remote(src, dst, send, recv, peer):
        return pltpu.make_async_remote_copy(
            src_ref=src,
            dst_ref=dst,
            send_sem=send,
            recv_sem=recv,
            device_id=peer,
            device_id_type=pl.DeviceIdType.MESH,
        )

    def load_a(g):
        cut = pl.ds(g * 4, 4)
        return pltpu.make_async_copy(a_hbm.at[cut], a_buf.at[cut], sem_a.at[g])

    def load_p(g):
        cut = pl.ds(g * 8, 8)
        return pltpu.make_async_copy(p_hbm.at[cut], p_buf.at[cut], sem_p.at[g])

    load_p(0).start()
    load_a(0).start()
    load_a(1).start()
    load_p(7).start()
    for g in range(1, 7):
        load_p(g).start()
        load_a(g + 1).start()

    nxt, prv = ring_peer(1), ring_peer(255)
    barrier = pltpu.get_barrier_semaphore()
    with jax.named_scope("signals"):
        for peer in [nxt, prv] + [dev_peer(k) for k in range(1, 16)] + [grp_peer(k) for k in range(1, 16)]:
            pl.semaphore_signal(barrier, inc=1, device_id=peer, device_id_type=pl.DeviceIdType.MESH)

    zero_f = jnp.zeros((T, T), F32)
    zero_b = jnp.zeros((T, T), BF16)
    prod[PZ] = zero_f
    p_buf[64] = zero_f
    pt[64] = zero_b
    pt[129] = zero_b
    for side, block in ((0, 0), (1, NB - 1)):
        for slot in range(2):
            id_send[side, :, slot * T : (slot + 1) * T] = jnp.full((8, T), ids[slot, block], jnp.int32)

    def pick(block, j, first, none):
        return jnp.where(ids[0, block] == j, first, jnp.where(ids[1, block] == j, first + 1, none))

    def push_p(p0, p1, unit):
        h0, l0 = split(p0)
        h1, l1 = split(p1)
        high, low = jnp.concatenate([h0, h1], axis=1), jnp.concatenate([l0, l1], axis=1)
        pltpu.matmul_push_rhs(jnp.concatenate([high, low], axis=0), 0, unit)
        return (h0, h1), (l0, l1)

    def gather(n0, n1, n2, j, ends):
        total = prod[pick(n1, j, n1 * 6 + 2, PZ)]
        if ends != 0:
            total = total + prod[pick(n0, j, n0 * 6, PZ)]
        if ends != 1:
            total = total + prod[pick(n2, j, n2 * 6 + 4, PZ)]
        return total

    def put_r(pair, half, j, value):
        r2[pair, 0, j, half * T : (half + 1) * T] = value
        r2[pair, 1, j, half * T : (half + 1) * T] = rest(value)

    def assemble(pair):
        for half in range(2):
            block = pair * 2 - 1 + half
            low = jnp.maximum(block - 1, 0)
            mid = jnp.maximum(block, 0)
            for j in range(CT):
                put_r(pair, half, j, gather(low, mid, block + 1, j, None))

    def body(acc, odd, tot):

        def products(t, into):
            for unit in range(2):
                n = t * 2 + unit
                high, low = push_p(p_buf[n * 2], p_buf[n * 2 + 1], unit)
                for slot in range(2):
                    pt[n * 2 + slot] = high[slot].T
                    pt[65 + n * 2 + slot] = low[slot].T
                for m in range(3):
                    tile = a_buf[jnp.clip(n + 1 - m, 0, NB - 1), m]
                    pltpu.matmul_acc_lhs(into[unit][m], twice(tile), load_staged_rhs=0 if m == 0 else None)
                    pltpu.matmul_acc_lhs(into[unit][m], twice(rest(tile)))

        def drain(t, into):
            for unit in range(2):
                n = t * 2 + unit
                for m in range(3):
                    res = pltpu.matmul_pop(into[unit][m])
                    prod[(n * 3 + m) * 2] = res[:, :T]
                    prod[(n * 3 + m) * 2 + 1] = res[:, T:]

        def steps(t):
            products(t, acc)
            products(t + 1, odd)
            assemble(jnp.maximum(t - 1, 0))
            drain(t, acc)
            assemble(t)
            drain(t + 1, odd)

        with jax.named_scope("load"):
            load_p(0).wait()
            load_a(0).wait()
            load_a(1).wait()
        with jax.named_scope("two_steps"):
            steps(0)
        with jax.named_scope("load7"):
            load_p(7).wait()
        with jax.named_scope("barrier"):
            pl.semaphore_wait(barrier, 32)
        halo_copies = [
            remote(p_buf.at[pl.ds(62, 2)], halo.at[0], sem_hs.at[0], sem_hr.at[0], nxt),
            remote(p_buf.at[pl.ds(0, 2)], halo.at[1], sem_hs.at[1], sem_hr.at[1], prv),
            remote(id_send.at[1], halo_id.at[0], sem_hs.at[2], sem_hr.at[2], nxt),
            remote(id_send.at[0], halo_id.at[1], sem_hs.at[3], sem_hr.at[3], prv),
        ]
        for copy in halo_copies:
            copy.start()

        def later_group(g, carry):
            load_p(g).wait()
            load_a(g + 1).wait()
            steps(g * 2)
            return carry

        with jax.named_scope("right_loop"):
            lax.fori_loop(1, 7, later_group, 0)
        with jax.named_scope("right_end"):
            steps(14)
            assemble(15)

        with jax.named_scope("halo_wait"):
            for copy in halo_copies:
                copy.wait_recv()
        for side in range(2):
            push_p(halo[side, 0], halo[side, 1], side)
            tile = a_buf[0, 0] if side == 0 else a_buf[NB - 1, 2]
            pltpu.matmul_acc_lhs(acc[side][0], twice(tile), load_staged_rhs=0)
            pltpu.matmul_acc_lhs(acc[side][0], twice(rest(tile)))
        edge = [pltpu.matmul_pop(acc[side][0]) for side in range(2)]
        for side in range(2):
            prod[193 + side * 2] = edge[side][:, :T]
            prod[194 + side * 2] = edge[side][:, T:]
        inner = [dev > 0, dev < 15]
        for half, side in ((0, 1), (1, 0)):
            for j in range(CT):
                own = gather(30, 31, 31, j, 1) if side == 1 else gather(0, 0, 1, j, 0)
                extra = zero_f
                for slot in range(2):
                    match = halo_id[side, 0:1, slot * T : (slot + 1) * T] == j
                    extra = extra + jnp.where(match, prod[193 + side * 2 + slot], 0.0)
                put_r(0, half, j, own + jnp.where(inner[side], extra, 0.0))

        def lhs(b0, b1, i, low):
            base = 65 if low else 0
            none = 129 if low else 64
            return jnp.concatenate(
                [pt[pick(b0, i, base + b0 * 2, none)], pt[pick(b1, i, base + b1 * 2, none)]], axis=1
            )

        ends = ((0, 0), (1, 15))

        def edge_y(side, rel):
            other = lax.rem(dy + rel, 4)
            return remote(
                e_send.at[side, other], e_y.at[side], sem_es.at[side, rel - 1], sem_er.at[side, 0], y_peer(rel)
            )

        def edge_z(side, rel):
            other = lax.rem(dz + rel, 4)
            return remote(
                e_pass.at[side, other], e_recv.at[side], sem_es.at[side, rel + 2], sem_er.at[side, 1], z_peer(rel)
            )

        for side, at in ends:

            @pl.when(dev == at)
            def _(side=side, at=at):
                block = 0 if side == 0 else NB - 1
                y0, y1 = prod[193 + side * 2], prod[194 + side * 2]
                wide = jnp.concatenate([y0, y1], axis=1)
                for part in (wide, rest(wide)):
                    for unit in range(2):
                        pltpu.matmul_push_rhs(jnp.concatenate([part, part], axis=0), 0, unit)
                        left = jnp.concatenate([pt[block * 2 + unit], pt[65 + block * 2 + unit]], axis=1)
                        pltpu.matmul_acc_lhs(acc[unit][0], left, load_staged_rhs=0)
                for unit in range(2):
                    res = pltpu.matmul_pop(acc[unit][0])
                    for y in range(4):
                        e_send[side, y, unit * 32 : (unit + 1) * 32] = res[y * 32 : (y + 1) * 32]
                upper = lax.broadcasted_iota(jnp.int32, (8, 2 * T), 0) < 4
                code = jnp.where(upper, halo_id[side], id_send[side]).astype(F32)
                for y in range(4):
                    e_send[side, y, 64:72] = code
                for rel in range(1, 4):
                    edge_y(side, rel).start()
                e_y[side] = e_send[side, at % 4]

        def pass_edges():
            for side, at in ends:

                @pl.when(dz == at // 4)
                def _(side=side, at=at):
                    @pl.when(dy != at % 4)
                    def _():
                        edge_y(side, 1).wait_recv()

                    for z in range(4):
                        for part in range(2):
                            half = slice(part * T, (part + 1) * T)
                            value = jnp.zeros((32, T), F32)
                            for slot in range(2):
                                match = e_y[side, 68:69, slot * T : (slot + 1) * T] == float(z)
                                value = value + jnp.where(match, e_y[side, slot * 32 : (slot + 1) * 32, half], 0.0)
                            e_pass[side, z, 0:32, half] = value
                        e_pass[side, z, 32:40] = e_y[side, 64:72]
                    for rel in range(1, 4):
                        edge_z(side, rel).start()
                    e_recv[side] = e_pass[side, at // 4]

        def totals(chunk, between):
            def right(pair, part):
                return jnp.concatenate([r2[pair, part, chunk * 2], r2[pair, part, chunk * 2 + 1]], axis=1)

            def pair_step(pair, b0, b1):
                for unit in range(2):
                    rows = (unit * 2, unit * 2 + 1)
                    high = jnp.concatenate([lhs(b0, b1, i, False) for i in rows], axis=0)
                    low = jnp.concatenate([lhs(b0, b1, i, True) for i in rows], axis=0)
                    pltpu.matmul_push_rhs(right(pair, 0), 0, unit)
                    pltpu.matmul_push_rhs(right(pair, 1), 1, unit)
                    pltpu.matmul_acc_lhs(tot[unit], high, load_staged_rhs=0)
                    pltpu.matmul_acc_lhs(tot[unit], low)
                    pltpu.matmul_acc_lhs(tot[unit], high, load_staged_rhs=1)

            def dots(pair, b0, b1, total):
                for half, block in ((0, b0), (1, b1)):
                    for j in range(CT):
                        both = r2[pair, 0, j, half * T : (half + 1) * T] * p_buf[pick(block, j, block * 2, 64)]
                        total = total + jnp.sum(both.reshape(16, 8, T), axis=0)
                return total

            def several(k, total):
                for u in range(3):
                    pair = k * 3 + 1 + u
                    pair_step(pair, pair * 2 - 1, pair * 2)
                    if chunk == 0:
                        total = dots(pair, pair * 2 - 1, pair * 2, total)
                return total

            total = jnp.zeros((8, T), F32)
            for k, (first, last) in enumerate(((0, 2), (2, 5))):
                with jax.named_scope("left_loop"):
                    total = lax.fori_loop(first, last, several, total)
                if k == 0:
                    between()
            pair_step(0, NB - 1, 0)
            if chunk == 0:
                total = dots(0, NB - 1, 0, total)
            for unit in range(2):
                res = pltpu.matmul_pop(tot[unit])
                for half in range(2):
                    i = unit * 2 + half
                    for y in range(4):
                        c_send[chunk, y, i] = res[half * T + y * 32 : half * T + (y + 1) * 32]
            return total

        up, down = lax.rem(dy + 1, 4), lax.rem(dy + 3, 4)
        far = lax.rem(dy + 2, 4)
        lo2, hi2 = pl.ds(0, 2), pl.ds(2, 2)

        def y_first(c):
            return [
                remote(c_send.at[c, far, lo2], y_a.at[c, 0], sem_ys.at[c, 0], sem_yr.at[c, 0], y_peer(1)),
                remote(c_send.at[c, far, hi2], y_a.at[c, 1], sem_ys.at[c, 1], sem_yr.at[c, 1], y_peer(3)),
                remote(c_send.at[c, up, hi2], y_d.at[c, 0], sem_ys.at[c, 2], sem_yr.at[c, 2], y_peer(1)),
                remote(c_send.at[c, down, lo2], y_d.at[c, 1], sem_ys.at[c, 3], sem_yr.at[c, 3], y_peer(3)),
            ]

        def y_second(c):
            return [
                remote(c_send.at[c, up, lo2], y_b.at[c, 0], sem_ys.at[c, 4], sem_yr.at[c, 4], y_peer(1)),
                remote(c_send.at[c, down, hi2], y_b.at[c, 1], sem_ys.at[c, 5], sem_yr.at[c, 5], y_peer(3)),
            ]

        z_up, z_down, z_far = lax.rem(dz + 1, 4), lax.rem(dz + 3, 4), lax.rem(dz + 2, 4)
        top, low16 = pl.ds(0, 16), pl.ds(16, 16)

        def z_first(c):
            return [
                remote(z_send.at[c, z_far, top], z_a.at[c, 0], sem_zs.at[c, 0], sem_zr.at[c, 0], z_peer(1)),
                remote(z_send.at[c, z_far, low16], z_a.at[c, 1], sem_zs.at[c, 1], sem_zr.at[c, 1], z_peer(3)),
                remote(z_send.at[c, z_up, low16], z_d.at[c, 0], sem_zs.at[c, 2], sem_zr.at[c, 2], z_peer(1)),
                remote(z_send.at[c, z_down, top], z_d.at[c, 1], sem_zs.at[c, 3], sem_zr.at[c, 3], z_peer(3)),
            ]

        def z_second(c):
            return [
                remote(z_send.at[c, z_up, top], z_b.at[c, 0], sem_zs.at[c, 4], sem_zr.at[c, 4], z_peer(1)),
                remote(z_send.at[c, z_down, low16], z_b.at[c, 1], sem_zs.at[c, 5], sem_zr.at[c, 5], z_peer(3)),
            ]

        def begin_second(c):
            first = y_first(c)
            first[0].wait_recv()
            c_send[c, up, lo2] = c_send[c, up, lo2] + y_a[c, 0]
            y_second(c)[0].start()
            first[1].wait_recv()
            c_send[c, down, hi2] = c_send[c, down, hi2] + y_a[c, 1]
            y_second(c)[1].start()

        def begin_z(c):
            for copy in y_first(c)[2:] + y_second(c):
                copy.wait_recv()
            z_send[c, 0:2] = c_send[c, dy, lo2] + y_b[c, 0] + y_d[c, 1]
            z_send[c, 2:4] = c_send[c, dy, hi2] + y_b[c, 1] + y_d[c, 0]
            for copy in z_first(c):
                copy.start()

        def second_z(c):
            first = z_first(c)
            first[0].wait_recv()
            z_send[c, z_up, top] = z_send[c, z_up, top] + z_a[c, 0]
            z_second(c)[0].start()
            first[1].wait_recv()
            z_send[c, z_down, low16] = z_send[c, z_down, low16] + z_a[c, 1]
            z_second(c)[1].start()

        def t_copies(phase):
            into = t_one if phase == 0 else t_two
            peer = dev_peer if phase == 0 else grp_peer
            return [
                remote(t_send.at[phase], into.at[rel], sem_ts.at[phase, rel], sem_tr.at[phase, rel], peer(rel))
                for rel in range(1, 16)
            ]

        one, two = t_copies(0), t_copies(1)

        def start(copies):
            for copy in copies:
                copy.start()

        total = totals(0, lambda: None)
        t_send[0] = total
        start(y_first(0)[:2])
        start(one)

        def between():
            start(y_first(0)[2:])
            pass_edges()

        totals(1, between)
        start(y_first(1)[:2])
        with jax.named_scope("y_second_0"):
            begin_second(0)
        start(y_first(1)[2:])
        with jax.named_scope("trace_dev"):
            for rel in range(1, 16):
                one[rel - 1].wait_recv()
                total = total + t_one[rel]
            t_send[1] = total
            start(two)
        with jax.named_scope("y_second_1"):
            begin_second(1)
        with jax.named_scope("z_0"):
            begin_z(0)
        with jax.named_scope("z_1"):
            begin_z(1)
        with jax.named_scope("z_second_0"):
            second_z(0)
        with jax.named_scope("z_second_1"):
            second_z(1)
        with jax.named_scope("trace_grp"):
            for rel in range(1, 16):
                two[rel - 1].wait_recv()
                total = total + t_two[rel]
        mean = jnp.sum(total, axis=(0, 1), keepdims=True) * (1.0 / 8192.0)
        scale = jnp.broadcast_to(mean, (32, 2 * T))

        for side, at in ends:
            base = 0 if side == 0 else 1024

            with jax.named_scope("edge_wait"):

                @pl.when(dz != at // 4)
                def _(side=side):
                    edge_z(side, 1).wait_recv()

            for j in range(CT):
                value = jnp.zeros((32, T), F32)
                for slot in range(2):
                    match = e_recv[side, 32:33, slot * T : (slot + 1) * T] == float(j)
                    value = value + jnp.where(match, e_recv[side, 0:32, slot * T : (slot + 1) * T], 0.0)
                out[:, base + j * T : base + (j + 1) * T] = value / scale[:, :T]

        for c in range(2):
            with jax.named_scope("z_wait"):
                for copy in z_first(c)[2:] + z_second(c):
                    copy.wait_recv()
            value = jnp.concatenate(
                [
                    z_send[c, dz, top] + z_b[c, 0] + z_d[c, 1],
                    z_send[c, dz, low16] + z_b[c, 1] + z_d[c, 0],
                ],
                axis=0,
            )
            out[:, 512 + c * 256 : 512 + (c + 1) * 256] = value / scale

        done = jax.named_scope("sends_done")
        done.__enter__()
        for copy in halo_copies + one + two:
            copy.wait_send()
        for c in range(2):
            for copy in y_first(c) + y_second(c) + z_first(c) + z_second(c):
                copy.wait_send()
        for side, at in ends:

            @pl.when(dev == at)
            def _(side=side):
                for rel in range(1, 4):
                    edge_y(side, rel).wait_send()

            @pl.when(dz == at // 4)
            def _(side=side):
                for rel in range(1, 4):
                    edge_z(side, rel).wait_send()

        done.__exit__(None, None, None)

    small, other = (
        tuple(tuple(pltpu.ACC(unit)((T, 2 * T), F32) for _ in range(3)) for unit in range(2)) for _ in range(2)
    )
    large = tuple(pltpu.ACC(unit)((2 * T, 2 * T), F32) for unit in range(2))
    pl.run_scoped(body, small, other, large)


def local(a_tiles, prolong, coarse_ids):
    vmem, dma = pltpu.VMEM, pltpu.SemaphoreType.DMA
    return pl.pallas_call(
        kernel,
        out_shape=jax.ShapeDtypeStruct((32, 1536), F32),
        in_specs=[
            pl.BlockSpec(memory_space=pltpu.SMEM),
            pl.BlockSpec(memory_space=pltpu.HBM),
            pl.BlockSpec(memory_space=pltpu.HBM),
        ],
        out_specs=pl.BlockSpec(memory_space=pltpu.VMEM),
        scratch_shapes=[
            vmem((NB, 3, T, T), F32),
            vmem((65, T, T), F32),
            vmem((130, T, T), BF16),
            vmem((197, T, T), F32),
            vmem((16, 2, 4, 2 * T, T), F32),
            vmem((2, 2, T, T), F32),
            vmem((2, 8, 2 * T), jnp.int32),
            vmem((2, 8, 2 * T), jnp.int32),
            vmem((2, 4, 4, 32, 2 * T), F32),
            vmem((2, 2, 2, 32, 2 * T), F32),
            vmem((2, 2, 2, 32, 2 * T), F32),
            vmem((2, 2, 2, 32, 2 * T), F32),
            vmem((2, 4, 32, 2 * T), F32),
            vmem((2, 2, 16, 2 * T), F32),
            vmem((2, 2, 16, 2 * T), F32),
            vmem((2, 2, 16, 2 * T), F32),
            vmem((2, 4, 72, 2 * T), F32),
            vmem((2, 72, 2 * T), F32),
            vmem((2, 4, 40, 2 * T), F32),
            vmem((2, 40, 2 * T), F32),
            vmem((2, 8, T), F32),
            vmem((16, 8, T), F32),
            vmem((16, 8, T), F32),
            dma((8,)),
            dma((8,)),
            dma((4,)),
            dma((4,)),
            dma((2, 6)),
            dma((2, 6)),
            dma((2, 6)),
            dma((2, 6)),
            dma((2, 6)),
            dma((2, 2)),
            dma((2, 16)),
            dma((2, 16)),
        ],
        compiler_params=pltpu.CompilerParams(
            collective_id=0, has_side_effects=True, vmem_limit_bytes=VMEM_MIB * 1024 * 1024
        ),
    )(coarse_ids.T, a_tiles, prolong.reshape(2 * NB, T, T))


def solution(mesh):
    torus = Mesh(mesh.devices.reshape(4, 2, 2, 4, 4), GRP_DEV)

    def run(a_tiles, prolong, coarse_ids):
        return jax.shard_map(
            local,
            mesh=torus,
            in_specs=(P(GRP_DEV, None, None, None), P(GRP_DEV, None, None, None), P(GRP_DEV, None)),
            out_specs=P(GRP_DEV, None),
            check_vma=False,
        )(a_tiles, prolong, coarse_ids)

    return run
```

time: 49.5 us -> 45.7 us (0.923)
  the two profiles are of different devices: /device:TPU:1 before, /device:TPU:2 now
where the time goes in v2:
time: 45.7 us; the launch traced here: 45.6 us
  Pallas kernels  44.2 us (97%)
  local copies, waits for them, and re-layouts  1.36 us (3%)
    pallas_call x1, Pallas kernels, local(): pl.pallas_call(kernel, out_shape=jax.ShapeDtypeStruct((32, 1536), F32), i...  44.2 us
    unnamed x3, local copies, waits for them, and re-layouts  1.36 us

profile of v2, /device:TPU:2, one launch (start us, length us, event | category | flops | bytes accessed | tf_op | source)
XLA Modules:
  0.0 45.6 jit_solution(3203248145337020319)
XLA Ops:
  0.0 0.0 copy-start
  0.0 0.7 %copy-done = s32[32,2]{0,1:T(2,128)S(1)} copy-done((s32[32,2]{0,1:T(2,128)S(1)}, s32[32,2]{0,1:T(2,128)}, u32[]{:S(2)}) %copy-start) | copy-done | bytes 280
  0.7 44.2 %shard_map.37 = f32[32,1536]{1,0:T(8,128)S(1)} custom-call(s32[2,32]{1,0:T(2,128)S(1)} %bitcast.2, f32[32,3,128,128]{3,2,1,0:T(8,128)} %a_hbm.1, f32[64,128,128]{2,1,0:T(8,128)} %bitcast.3), custom_call_target="tpu_custom_call" | custom-call | tf_op jit(solution)/shard_map/pallas_call | solution.py:544
  44.9 0.7 %copy.5 = f32[32,1536]{1,0:T(8,128)} copy(f32[32,1536]{1,0:T(8,128)S(1)} %shard_map.37) | data formatting | bytes 393216
Async XLA Ops:
  0.0 0.7 %copy-start = (s32[32,2]{0,1:T(2,128)S(1)}, s32[32,2]{0,1:T(2,128)}, u32[]{:S(2)}) copy-start(s32[32,2]{0,1:T(2,128)} %param.5) | copy-start | bytes 772

commit v3 on v2

--- a/solution.py
+++ b/solution.py
@@ -45,7 +45,8 @@
     p_buf,
     pt,
     prod,
-    r2,
+    r_even,
+    r_odd,
     halo,
     halo_id,
     id_send,
@@ -54,9 +55,7 @@
     y_b,
     y_d,
     z_send,
-    z_a,
-    z_b,
-    z_d,
+    z_recv,
     e_send,
     e_y,
     e_pass,
@@ -161,17 +160,24 @@
             total = total + prod[pick(n2, j, n2 * 6 + 4, PZ)]
         return total
 
-    def put_r(pair, half, j, value):
-        r2[pair, 0, j, half * T : (half + 1) * T] = value
-        r2[pair, 1, j, half * T : (half + 1) * T] = rest(value)
-
-    def assemble(pair):
+    def r_at(pair, parity):
+        return (r_even, r_odd)[parity].at[pair // 2]
+
+    def put_r(pair, parity, half, j, value, block):
+        into = r_at(pair, parity)
+        into[0, j, half * T : (half + 1) * T] = value
+        into[1, j, half * T : (half + 1) * T] = rest(value)
+        both = value * p_buf[pick(block, j, block * 2, 64)]
+        return jnp.sum(both.reshape(16, 8, T), axis=0)
+
+    def assemble(pair, parity):
+        total = jnp.zeros((8, T), F32)
         for half in range(2):
             block = pair * 2 - 1 + half
-            low = jnp.maximum(block - 1, 0)
-            mid = jnp.maximum(block, 0)
             for j in range(CT):
-                put_r(pair, half, j, gather(low, mid, block + 1, j, None))
+                value = gather(block - 1, block, block + 1, j, None)
+                total = total + put_r(pair, parity, half, j, value, block)
+        return total
 
     def body(acc, odd, tot):
 
@@ -195,22 +201,36 @@
                     prod[(n * 3 + m) * 2] = res[:, :T]
                     prod[(n * 3 + m) * 2 + 1] = res[:, T:]
 
-        def steps(t):
+        def one_group(g):
+            products(g * 2, acc)
+            products(g * 2 + 1, odd)
+            drain(g * 2, acc)
+            drain(g * 2 + 1, odd)
+
+        def two_groups(k, carry):
+            for u in (1, 2):
+                load_p(k * 2 + u).wait()
+                load_a(k * 2 + u + 1).wait()
+            t = k * 4 + 2
             products(t, acc)
             products(t + 1, odd)
-            assemble(jnp.maximum(t - 1, 0))
             drain(t, acc)
-            assemble(t)
+            products(t + 2, acc)
             drain(t + 1, odd)
+            products(t + 3, odd)
+            drain(t + 2, acc)
+            drain(t + 3, odd)
+            return carry
 
         with jax.named_scope("load"):
             load_p(0).wait()
             load_a(0).wait()
             load_a(1).wait()
-        with jax.named_scope("two_steps"):
-            steps(0)
-        with jax.named_scope("load7"):
-            load_p(7).wait()
+        with jax.named_scope("right_start"):
+            one_group(0)
+        with jax.named_scope("right_loop"):
+            lax.fori_loop(0, 2, two_groups, 0)
+        load_p(7).wait()
         with jax.named_scope("barrier"):
             pl.semaphore_wait(barrier, 32)
         halo_copies = [
@@ -221,18 +241,67 @@
         ]
         for copy in halo_copies:
             copy.start()
-
-        def later_group(g, carry):
-            load_p(g).wait()
-            load_a(g + 1).wait()
-            steps(g * 2)
+        with jax.named_scope("right_loop"):
+            lax.fori_loop(2, 3, two_groups, 0)
+        with jax.named_scope("right_end"):
+            one_group(7)
+
+        ends = ((0, 0), (1, 15))
+
+        def lhs(b0, b1, i, low):
+            base = 65 if low else 0
+            none = 129 if low else 64
+            return jnp.concatenate(
+                [pt[pick(b0, i, base + b0 * 2, none)], pt[pick(b1, i, base + b1 * 2, none)]], axis=1
+            )
+
+        def pair_step(chunk, pair, parity, b0, b1):
+            read = r_at(pair, parity)
+
+            def right(part):
+                return jnp.concatenate([read[part, chunk * 2], read[part, chunk * 2 + 1]], axis=1)
+
+            for unit in range(2):
+                rows = (unit * 2, unit * 2 + 1)
+                high = jnp.concatenate([lhs(b0, b1, i, False) for i in rows], axis=0)
+                low = jnp.concatenate([lhs(b0, b1, i, True) for i in rows], axis=0)
+                pltpu.matmul_push_rhs(right(0), 0, unit)
+                pltpu.matmul_push_rhs(right(1), 1, unit)
+                pltpu.matmul_acc_lhs(tot[unit], high, load_staged_rhs=0)
+                pltpu.matmul_acc_lhs(tot[unit], low)
+                pltpu.matmul_acc_lhs(tot[unit], high, load_staged_rhs=1)
+
+        def finish(chunk):
+            for unit in range(2):
+                res = pltpu.matmul_pop(tot[unit])
+                for half in range(2):
+                    i = unit * 2 + half
+                    for y in range(4):
+                        c_send[chunk, y, i] = res[half * T + y * 32 : half * T + (y + 1) * 32]
+
+        def four_first(k, total):
+            for u in range(4):
+                pair = k * 4 + 1 + u
+                pair_step(0, pair, (1 + u) % 2, pair * 2 - 1, pair * 2)
+                total = total + assemble(pair + 1, u % 2)
+            return total
+
+        def four_second(k, carry):
+            for u in range(4):
+                pair = k * 4 + 1 + u
+                pair_step(1, pair, (1 + u) % 2, pair * 2 - 1, pair * 2)
             return carry
 
-        with jax.named_scope("right_loop"):
-            lax.fori_loop(1, 7, later_group, 0)
-        with jax.named_scope("right_end"):
-            steps(14)
-            assemble(15)
+        with jax.named_scope("assemble"):
+            total = assemble(1, 1)
+        with jax.named_scope("left_loop_0"):
+            total = lax.fori_loop(0, 3, four_first, total)
+        with jax.named_scope("left_end_0"):
+            pair_step(0, 13, 1, 25, 26)
+            total = total + assemble(14, 0)
+            pair_step(0, 14, 0, 27, 28)
+            total = total + assemble(15, 1)
+            pair_step(0, 15, 1, 29, 30)
 
         with jax.named_scope("halo_wait"):
             for copy in halo_copies:
@@ -254,16 +323,12 @@
                 for slot in range(2):
                     match = halo_id[side, 0:1, slot * T : (slot + 1) * T] == j
                     extra = extra + jnp.where(match, prod[193 + side * 2 + slot], 0.0)
-                put_r(0, half, j, own + jnp.where(inner[side], extra, 0.0))
-
-        def lhs(b0, b1, i, low):
-            base = 65 if low else 0
-            none = 129 if low else 64
-            return jnp.concatenate(
-                [pt[pick(b0, i, base + b0 * 2, none)], pt[pick(b1, i, base + b1 * 2, none)]], axis=1
-            )
-
-        ends = ((0, 0), (1, 15))
+                block = 0 if half == 1 else NB - 1
+                total = total + put_r(0, 0, half, j, own + jnp.where(inner[side], extra, 0.0), block)
+
+        pair_step(0, 0, 0, NB - 1, 0)
+        finish(0)
+
 
         def edge_y(side, rel):
             other = lax.rem(dy + rel, 4)
@@ -277,29 +342,30 @@
                 e_pass.at[side, other], e_recv.at[side], sem_es.at[side, rel + 2], sem_er.at[side, 1], z_peer(rel)
             )
 
-        for side, at in ends:
-
-            @pl.when(dev == at)
-            def _(side=side, at=at):
-                block = 0 if side == 0 else NB - 1
-                y0, y1 = prod[193 + side * 2], prod[194 + side * 2]
-                wide = jnp.concatenate([y0, y1], axis=1)
-                for part in (wide, rest(wide)):
+        def start_edges():
+            for side, at in ends:
+
+                @pl.when(dev == at)
+                def _(side=side, at=at):
+                    block = 0 if side == 0 else NB - 1
+                    y0, y1 = prod[193 + side * 2], prod[194 + side * 2]
+                    wide = jnp.concatenate([y0, y1], axis=1)
+                    for part in (wide, rest(wide)):
+                        for unit in range(2):
+                            pltpu.matmul_push_rhs(jnp.concatenate([part, part], axis=0), 0, unit)
+                            left = jnp.concatenate([pt[block * 2 + unit], pt[65 + block * 2 + unit]], axis=1)
+                            pltpu.matmul_acc_lhs(acc[unit][0], left, load_staged_rhs=0)
                     for unit in range(2):
-                        pltpu.matmul_push_rhs(jnp.concatenate([part, part], axis=0), 0, unit)
-                        left = jnp.concatenate([pt[block * 2 + unit], pt[65 + block * 2 + unit]], axis=1)
-                        pltpu.matmul_acc_lhs(acc[unit][0], left, load_staged_rhs=0)
-                for unit in range(2):
-                    res = pltpu.matmul_pop(acc[unit][0])
+                        res = pltpu.matmul_pop(acc[unit][0])
+                        for y in range(4):
+                            e_send[side, y, unit * 32 : (unit + 1) * 32] = res[y * 32 : (y + 1) * 32]
+                    upper = lax.broadcasted_iota(jnp.int32, (8, 2 * T), 0) < 4
+                    code = jnp.where(upper, halo_id[side], id_send[side]).astype(F32)
                     for y in range(4):
-                        e_send[side, y, unit * 32 : (unit + 1) * 32] = res[y * 32 : (y + 1) * 32]
-                upper = lax.broadcasted_iota(jnp.int32, (8, 2 * T), 0) < 4
-                code = jnp.where(upper, halo_id[side], id_send[side]).astype(F32)
-                for y in range(4):
-                    e_send[side, y, 64:72] = code
-                for rel in range(1, 4):
-                    edge_y(side, rel).start()
-                e_y[side] = e_send[side, at % 4]
+                        e_send[side, y, 64:72] = code
+                    for rel in range(1, 4):
+                        edge_y(side, rel).start()
+                    e_y[side] = e_send[side, at % 4]
 
         def pass_edges():
             for side, at in ends:
@@ -323,53 +389,6 @@
                         edge_z(side, rel).start()
                     e_recv[side] = e_pass[side, at // 4]
 
-        def totals(chunk, between):
-            def right(pair, part):
-                return jnp.concatenate([r2[pair, part, chunk * 2], r2[pair, part, chunk * 2 + 1]], axis=1)
-
-            def pair_step(pair, b0, b1):
-                for unit in range(2):
-                    rows = (unit * 2, unit * 2 + 1)
-                    high = jnp.concatenate([lhs(b0, b1, i, False) for i in rows], axis=0)
-                    low = jnp.concatenate([lhs(b0, b1, i, True) for i in rows], axis=0)
-                    pltpu.matmul_push_rhs(right(pair, 0), 0, unit)
-                    pltpu.matmul_push_rhs(right(pair, 1), 1, unit)
-                    pltpu.matmul_acc_lhs(tot[unit], high, load_staged_rhs=0)
-                    pltpu.matmul_acc_lhs(tot[unit], low)
-                    pltpu.matmul_acc_lhs(tot[unit], high, load_staged_rhs=1)
-
-            def dots(pair, b0, b1, total):
-                for half, block in ((0, b0), (1, b1)):
-                    for j in range(CT):
-                        both = r2[pair, 0, j, half * T : (half + 1) * T] * p_buf[pick(block, j, block * 2, 64)]
-                        total = total + jnp.sum(both.reshape(16, 8, T), axis=0)
-                return total
-
-            def several(k, total):
-                for u in range(3):
-                    pair = k * 3 + 1 + u
-                    pair_step(pair, pair * 2 - 1, pair * 2)
-                    if chunk == 0:
-                        total = dots(pair, pair * 2 - 1, pair * 2, total)
-                return total
-
-            total = jnp.zeros((8, T), F32)
-            for k, (first, last) in enumerate(((0, 2), (2, 5))):
-                with jax.named_scope("left_loop"):
-                    total = lax.fori_loop(first, last, several, total)
-                if k == 0:
-                    between()
-            pair_step(0, NB - 1, 0)
-            if chunk == 0:
-                total = dots(0, NB - 1, 0, total)
-            for unit in range(2):
-                res = pltpu.matmul_pop(tot[unit])
-                for half in range(2):
-                    i = unit * 2 + half
-                    for y in range(4):
-                        c_send[chunk, y, i] = res[half * T + y * 32 : half * T + (y + 1) * 32]
-            return total
-
         up, down = lax.rem(dy + 1, 4), lax.rem(dy + 3, 4)
         far = lax.rem(dy + 2, 4)
         lo2, hi2 = pl.ds(0, 2), pl.ds(2, 2)
@@ -388,21 +407,16 @@
                 remote(c_send.at[c, down, hi2], y_b.at[c, 1], sem_ys.at[c, 5], sem_yr.at[c, 5], y_peer(3)),
             ]
 
-        z_up, z_down, z_far = lax.rem(dz + 1, 4), lax.rem(dz + 3, 4), lax.rem(dz + 2, 4)
-        top, low16 = pl.ds(0, 16), pl.ds(16, 16)
-
-        def z_first(c):
+        def z_all(c):
             return [
-                remote(z_send.at[c, z_far, top], z_a.at[c, 0], sem_zs.at[c, 0], sem_zr.at[c, 0], z_peer(1)),
-                remote(z_send.at[c, z_far, low16], z_a.at[c, 1], sem_zs.at[c, 1], sem_zr.at[c, 1], z_peer(3)),
-                remote(z_send.at[c, z_up, low16], z_d.at[c, 0], sem_zs.at[c, 2], sem_zr.at[c, 2], z_peer(1)),
-                remote(z_send.at[c, z_down, top], z_d.at[c, 1], sem_zs.at[c, 3], sem_zr.at[c, 3], z_peer(3)),
-            ]
-
-        def z_second(c):
-            return [
-                remote(z_send.at[c, z_up, top], z_b.at[c, 0], sem_zs.at[c, 4], sem_zr.at[c, 4], z_peer(1)),
-                remote(z_send.at[c, z_down, low16], z_b.at[c, 1], sem_zs.at[c, 5], sem_zr.at[c, 5], z_peer(3)),
+                remote(
+                    z_send.at[c, lax.rem(dz + rel, 4)],
+                    z_recv.at[c, rel - 1],
+                    sem_zs.at[c, rel - 1],
+                    sem_zr.at[c, rel - 1],
+                    z_peer(rel),
+                )
+                for rel in range(1, 4)
             ]
 
         def begin_second(c):
@@ -419,23 +433,15 @@
                 copy.wait_recv()
             z_send[c, 0:2] = c_send[c, dy, lo2] + y_b[c, 0] + y_d[c, 1]
             z_send[c, 2:4] = c_send[c, dy, hi2] + y_b[c, 1] + y_d[c, 0]
-            for copy in z_first(c):
+            for copy in z_all(c):
                 copy.start()
-
-        def second_z(c):
-            first = z_first(c)
-            first[0].wait_recv()
-            z_send[c, z_up, top] = z_send[c, z_up, top] + z_a[c, 0]
-            z_second(c)[0].start()
-            first[1].wait_recv()
-            z_send[c, z_down, low16] = z_send[c, z_down, low16] + z_a[c, 1]
-            z_second(c)[1].start()
 
         def t_copies(phase):
             into = t_one if phase == 0 else t_two
+            row = pl.ds(0, 1)
             peer = dev_peer if phase == 0 else grp_peer
             return [
-                remote(t_send.at[phase], into.at[rel], sem_ts.at[phase, rel], sem_tr.at[phase, rel], peer(rel))
+                remote(t_send.at[phase, row], into.at[rel, row], sem_ts.at[phase, rel], sem_tr.at[phase, rel], peer(rel))
                 for rel in range(1, 16)
             ]
 
@@ -445,16 +451,21 @@
             for copy in copies:
                 copy.start()
 
-        total = totals(0, lambda: None)
-        t_send[0] = total
+        total = jnp.sum(total, axis=0, keepdims=True)
+        t_send[0, 0:1] = total
+        start(one)
         start(y_first(0)[:2])
-        start(one)
-
-        def between():
-            start(y_first(0)[2:])
-            pass_edges()
-
-        totals(1, between)
+        with jax.named_scope("edges"):
+            start_edges()
+        with jax.named_scope("left_loop_1"):
+            lax.fori_loop(0, 1, four_second, 0)
+        start(y_first(0)[2:])
+        with jax.named_scope("left_loop_1"):
+            lax.fori_loop(1, 3, four_second, 0)
+        for pair in (13, 14, 15):
+            pair_step(1, pair, pair % 2, pair * 2 - 1, pair * 2)
+        pair_step(1, 0, 0, NB - 1, 0)
+        finish(1)
         start(y_first(1)[:2])
         with jax.named_scope("y_second_0"):
             begin_second(0)
@@ -462,23 +473,21 @@
         with jax.named_scope("trace_dev"):
             for rel in range(1, 16):
                 one[rel - 1].wait_recv()
-                total = total + t_one[rel]
-            t_send[1] = total
+                total = total + t_one[rel, 0:1]
+            t_send[1, 0:1] = total
             start(two)
         with jax.named_scope("y_second_1"):
             begin_second(1)
+        with jax.named_scope("edge_pass"):
+            pass_edges()
         with jax.named_scope("z_0"):
             begin_z(0)
         with jax.named_scope("z_1"):
             begin_z(1)
-        with jax.named_scope("z_second_0"):
-            second_z(0)
-        with jax.named_scope("z_second_1"):
-            second_z(1)
         with jax.named_scope("trace_grp"):
             for rel in range(1, 16):
                 two[rel - 1].wait_recv()
-                total = total + t_two[rel]
+                total = total + t_two[rel, 0:1]
         mean = jnp.sum(total, axis=(0, 1), keepdims=True) * (1.0 / 8192.0)
         scale = jnp.broadcast_to(mean, (32, 2 * T))
 
@@ -499,16 +508,11 @@
                 out[:, base + j * T : base + (j + 1) * T] = value / scale[:, :T]
 
         for c in range(2):
+            value = z_send[c, dz]
             with jax.named_scope("z_wait"):
-                for copy in z_first(c)[2:] + z_second(c):
+                for k, copy in enumerate(z_all(c)):
                     copy.wait_recv()
-            value = jnp.concatenate(
-                [
-                    z_send[c, dz, top] + z_b[c, 0] + z_d[c, 1],
-                    z_send[c, dz, low16] + z_b[c, 1] + z_d[c, 0],
-                ],
-                axis=0,
-            )
+                    value = value + z_recv[c, k]
             out[:, 512 + c * 256 : 512 + (c + 1) * 256] = value / scale
 
         done = jax.named_scope("sends_done")
@@ -516,7 +520,7 @@
         for copy in halo_copies + one + two:
             copy.wait_send()
         for c in range(2):
-            for copy in y_first(c) + y_second(c) + z_first(c) + z_second(c):
+            for copy in y_first(c) + y_second(c) + z_all(c):
                 copy.wait_send()
         for side, at in ends:
 
@@ -555,7 +559,8 @@
             vmem((65, T, T), F32),
             vmem((130, T, T), BF16),
             vmem((197, T, T), F32),
-            vmem((16, 2, 4, 2 * T, T), F32),
+            vmem((8, 2, 4, 2 * T, T), F32),
+            vmem((8, 2, 4, 2 * T, T), F32),
             vmem((2, 2, T, T), F32),
             vmem((2, 8, 2 * T), jnp.int32),
             vmem((2, 8, 2 * T), jnp.int32),
@@ -564,9 +569,7 @@
             vmem((2, 2, 2, 32, 2 * T), F32),
             vmem((2, 2, 2, 32, 2 * T), F32),
             vmem((2, 4, 32, 2 * T), F32),
-            vmem((2, 2, 16, 2 * T), F32),
-            vmem((2, 2, 16, 2 * T), F32),
-            vmem((2, 2, 16, 2 * T), F32),
+            vmem((2, 3, 32, 2 * T), F32),
             vmem((2, 4, 72, 2 * T), F32),
             vmem((2, 72, 2 * T), F32),
             vmem((2, 4, 40, 2 * T), F32),

time: 45.7 us -> 41.3 us (0.904)
  the two profiles are of different devices: /device:TPU:2 before, /device:TPU:39 now
where the time goes in v3:
time: 41.3 us; the launch traced here: 41.2 us
  Pallas kernels  39.8 us (96%)
  local copies, waits for them, and re-layouts  1.36 us (3%)
    pallas_call x1, Pallas kernels, local(): pl.pallas_call(kernel, out_shape=jax.ShapeDtypeStruct((32, 1536), F32), i...  39.8 us
    unnamed x3, local copies, waits for them, and re-layouts  1.36 us

profile of v3, /device:TPU:39, one launch (start us, length us, event | category | flops | bytes accessed | tf_op | source)
XLA Modules:
  0.0 41.2 jit_solution(2711953771581951040)
XLA Ops:
  0.0 0.0 copy-start
  0.0 0.7 %copy-done = s32[32,2]{0,1:T(2,128)S(1)} copy-done((s32[32,2]{0,1:T(2,128)S(1)}, s32[32,2]{0,1:T(2,128)}, u32[]{:S(2)}) %copy-start) | copy-done | bytes 280
  0.7 39.8 %shard_map.37 = f32[32,1536]{1,0:T(8,128)S(1)} custom-call(s32[2,32]{1,0:T(2,128)S(1)} %bitcast.2, f32[32,3,128,128]{3,2,1,0:T(8,128)} %a_hbm.1, f32[64,128,128]{2,1,0:T(8,128)} %bitcast.3), custom_call_target="tpu_custom_call" | custom-call | tf_op jit(solution)/shard_map/pallas_call | solution.py:548
  40.5 0.7 %copy.5 = f32[32,1536]{1,0:T(8,128)} copy(f32[32,1536]{1,0:T(8,128)S(1)} %shard_map.37) | data formatting | bytes 393216
Async XLA Ops:
  0.0 0.7 %copy-start = (s32[32,2]{0,1:T(2,128)S(1)}, s32[32,2]{0,1:T(2,128)}, u32[]{:S(2)}) copy-start(s32[32,2]{0,1:T(2,128)} %param.5) | copy-start | bytes 772

commit v4 on v3

--- a/solution.py
+++ b/solution.py
@@ -12,6 +12,7 @@
 T = 128
 CT = 4
 PZ = 192
+OFFSETS = (2, 1, 3, 0)
 VMEM_MIB = 53
 F32 = jnp.float32
 BF16 = jnp.bfloat16
@@ -51,9 +52,7 @@
     halo_id,
     id_send,
     c_send,
-    y_a,
-    y_b,
-    y_d,
+    y_recv,
     z_send,
     z_recv,
     e_send,
@@ -61,8 +60,7 @@
     e_pass,
     e_recv,
     t_send,
-    t_one,
-    t_two,
+    t_recv,
     sem_a,
     sem_p,
     sem_hs,
@@ -128,8 +126,9 @@
 
     nxt, prv = ring_peer(1), ring_peer(255)
     barrier = pltpu.get_barrier_semaphore()
+    peers = [nxt, prv] + [dev_peer(k) for k in range(1, 16)] + [grp_peer(k) for k in range(1, 16)]
     with jax.named_scope("signals"):
-        for peer in [nxt, prv] + [dev_peer(k) for k in range(1, 16)] + [grp_peer(k) for k in range(1, 16)]:
+        for peer in peers:
             pl.semaphore_signal(barrier, inc=1, device_id=peer, device_id_type=pl.DeviceIdType.MESH)
 
     zero_f = jnp.zeros((T, T), F32)
@@ -152,34 +151,36 @@
         pltpu.matmul_push_rhs(jnp.concatenate([high, low], axis=0), 0, unit)
         return (h0, h1), (l0, l1)
 
-    def gather(n0, n1, n2, j, ends):
-        total = prod[pick(n1, j, n1 * 6 + 2, PZ)]
-        if ends != 0:
-            total = total + prod[pick(n0, j, n0 * 6, PZ)]
-        if ends != 1:
-            total = total + prod[pick(n2, j, n2 * 6 + 4, PZ)]
-        return total
-
     def r_at(pair, parity):
         return (r_even, r_odd)[parity].at[pair // 2]
 
-    def put_r(pair, parity, half, j, value, block):
+    def put_r(pair, parity, half, j, terms, block, extra=None):
         into = r_at(pair, parity)
-        into[0, j, half * T : (half + 1) * T] = value
-        into[1, j, half * T : (half + 1) * T] = rest(value)
-        both = value * p_buf[pick(block, j, block * 2, 64)]
-        return jnp.sum(both.reshape(16, 8, T), axis=0)
+        own = pick(block, j, block * 2, 64)
+        total = jnp.zeros((8, T), F32)
+        for k in range(4):
+            rows = pl.ds(k * 32, 32)
+            value = prod[terms[0], rows] + prod[terms[1], rows]
+            if len(terms) == 3:
+                value = value + prod[terms[2], rows]
+            if extra is not None:
+                value = value + extra[k * 32 : (k + 1) * 32]
+            place = pl.ds(half * T + k * 32, 32)
+            into[0, j, place] = value
+            into[1, j, place] = rest(value)
+            total = total + jnp.sum((value * p_buf[own, rows]).reshape(4, 8, T), axis=0)
+        return total
 
     def assemble(pair, parity):
         total = jnp.zeros((8, T), F32)
         for half in range(2):
             block = pair * 2 - 1 + half
             for j in range(CT):
-                value = gather(block - 1, block, block + 1, j, None)
-                total = total + put_r(pair, parity, half, j, value, block)
+                terms = [pick(block - 1 + m, j, (block - 1 + m) * 6 + m * 2, PZ) for m in range(3)]
+                total = total + put_r(pair, parity, half, j, terms, block)
         return total
 
-    def body(acc, odd, tot):
+    def body(acc, odd):
 
         def products(t, into):
             for unit in range(2):
@@ -229,7 +230,7 @@
         with jax.named_scope("right_start"):
             one_group(0)
         with jax.named_scope("right_loop"):
-            lax.fori_loop(0, 2, two_groups, 0)
+            lax.fori_loop(0, 1, two_groups, 0)
         load_p(7).wait()
         with jax.named_scope("barrier"):
             pl.semaphore_wait(barrier, 32)
@@ -242,7 +243,7 @@
         for copy in halo_copies:
             copy.start()
         with jax.named_scope("right_loop"):
-            lax.fori_loop(2, 3, two_groups, 0)
+            lax.fori_loop(1, 3, two_groups, 0)
         with jax.named_scope("right_end"):
             one_group(7)
 
@@ -255,29 +256,32 @@
                 [pt[pick(b0, i, base + b0 * 2, none)], pt[pick(b1, i, base + b1 * 2, none)]], axis=1
             )
 
-        def pair_step(chunk, pair, parity, b0, b1):
+        def pair_step(part, pair, parity, b0, b1):
             read = r_at(pair, parity)
-
-            def right(part):
-                return jnp.concatenate([read[part, chunk * 2], read[part, chunk * 2 + 1]], axis=1)
-
-            for unit in range(2):
-                rows = (unit * 2, unit * 2 + 1)
-                high = jnp.concatenate([lhs(b0, b1, i, False) for i in rows], axis=0)
-                low = jnp.concatenate([lhs(b0, b1, i, True) for i in rows], axis=0)
-                pltpu.matmul_push_rhs(right(0), 0, unit)
-                pltpu.matmul_push_rhs(right(1), 1, unit)
-                pltpu.matmul_acc_lhs(tot[unit], high, load_staged_rhs=0)
-                pltpu.matmul_acc_lhs(tot[unit], low)
-                pltpu.matmul_acc_lhs(tot[unit], high, load_staged_rhs=1)
-
-        def finish(chunk):
-            for unit in range(2):
-                res = pltpu.matmul_pop(tot[unit])
-                for half in range(2):
-                    i = unit * 2 + half
+            tiles = [lax.rem(dz + OFFSETS[part * 2 + t], 4) for t in range(2)]
+            high, low = ([lhs(b0, b1, i, under) for i in tiles] for under in (False, True))
+            into = (odd, acc)[part]
+
+            def push(level):
+                for unit in range(2):
+                    right = jnp.concatenate([read[level, unit * 2], read[level, unit * 2 + 1]], axis=1)
+                    pltpu.matmul_push_rhs(right, level, unit)
+
+            push(0)
+            for left, t, staged in ((low, 0, 0), (high, 0, None), (low, 1, None), (high, 1, None)):
+                for unit in range(2):
+                    pltpu.matmul_acc_lhs(into[unit][t], left[t], load_staged_rhs=staged)
+            push(1)
+            for left, t, staged in ((high, 1, 1), (high, 0, None)):
+                for unit in range(2):
+                    pltpu.matmul_acc_lhs(into[unit][t], left[t], load_staged_rhs=staged)
+
+        def finish(part):
+            for t in range(2):
+                for unit in range(2):
+                    res = pltpu.matmul_pop((odd, acc)[part][unit][t])
                     for y in range(4):
-                        c_send[chunk, y, i] = res[half * T + y * 32 : half * T + (y + 1) * 32]
+                        c_send[part * 2 + t, y, :, unit * 2 * T : (unit + 1) * 2 * T] = res[y * 32 : (y + 1) * 32]
 
         def four_first(k, total):
             for u in range(4):
@@ -288,8 +292,8 @@
 
         def four_second(k, carry):
             for u in range(4):
-                pair = k * 4 + 1 + u
-                pair_step(1, pair, (1 + u) % 2, pair * 2 - 1, pair * 2)
+                pair = lax.rem(k * 4 + 1 + u, 16)
+                pair_step(1, pair, (1 + u) % 2, lax.rem(pair * 2 + 31, 32), pair * 2)
             return carry
 
         with jax.named_scope("assemble"):
@@ -318,17 +322,14 @@
         inner = [dev > 0, dev < 15]
         for half, side in ((0, 1), (1, 0)):
             for j in range(CT):
-                own = gather(30, 31, 31, j, 1) if side == 1 else gather(0, 0, 1, j, 0)
+                block = 0 if half == 1 else NB - 1
+                terms = [pick(block, j, block * 6 + 2, PZ)]
+                terms += [pick(30, j, 180, PZ)] if side == 1 else [pick(1, j, 10, PZ)]
                 extra = zero_f
                 for slot in range(2):
                     match = halo_id[side, 0:1, slot * T : (slot + 1) * T] == j
                     extra = extra + jnp.where(match, prod[193 + side * 2 + slot], 0.0)
-                block = 0 if half == 1 else NB - 1
-                total = total + put_r(0, 0, half, j, own + jnp.where(inner[side], extra, 0.0), block)
-
-        pair_step(0, 0, 0, NB - 1, 0)
-        finish(0)
-
+                total = total + put_r(0, 0, half, j, terms, block, jnp.where(inner[side], extra, 0.0))
 
         def edge_y(side, rel):
             other = lax.rem(dy + rel, 4)
@@ -389,105 +390,89 @@
                         edge_z(side, rel).start()
                     e_recv[side] = e_pass[side, at // 4]
 
-        up, down = lax.rem(dy + 1, 4), lax.rem(dy + 3, 4)
-        far = lax.rem(dy + 2, 4)
-        lo2, hi2 = pl.ds(0, 2), pl.ds(2, 2)
-
-        def y_first(c):
-            return [
-                remote(c_send.at[c, far, lo2], y_a.at[c, 0], sem_ys.at[c, 0], sem_yr.at[c, 0], y_peer(1)),
-                remote(c_send.at[c, far, hi2], y_a.at[c, 1], sem_ys.at[c, 1], sem_yr.at[c, 1], y_peer(3)),
-                remote(c_send.at[c, up, hi2], y_d.at[c, 0], sem_ys.at[c, 2], sem_yr.at[c, 2], y_peer(1)),
-                remote(c_send.at[c, down, lo2], y_d.at[c, 1], sem_ys.at[c, 3], sem_yr.at[c, 3], y_peer(3)),
-            ]
-
-        def y_second(c):
-            return [
-                remote(c_send.at[c, up, lo2], y_b.at[c, 0], sem_ys.at[c, 4], sem_yr.at[c, 4], y_peer(1)),
-                remote(c_send.at[c, down, hi2], y_b.at[c, 1], sem_ys.at[c, 5], sem_yr.at[c, 5], y_peer(3)),
-            ]
-
-        def z_all(c):
+        def t_copies(phase):
+            row = pl.ds(0, 1)
+            peer = (dev_peer, grp_peer)[phase]
             return [
                 remote(
-                    z_send.at[c, lax.rem(dz + rel, 4)],
-                    z_recv.at[c, rel - 1],
-                    sem_zs.at[c, rel - 1],
-                    sem_zr.at[c, rel - 1],
-                    z_peer(rel),
+                    t_send.at[phase, row],
+                    t_recv.at[phase, rel, row],
+                    sem_ts.at[phase, rel],
+                    sem_tr.at[phase, rel],
+                    peer(rel),
+                )
+                for rel in range(1, 16)
+            ]
+
+        def t_begin(phase, total):
+            t_send[phase, 0:1] = total
+            start(t_copies(phase))
+
+        def t_sum(phase, total):
+            for rel, copy in enumerate(t_copies(phase)):
+                copy.wait_recv()
+                total = total + t_recv[phase, rel + 1, 0:1]
+            return total
+
+        def start(copies):
+            for copy in copies:
+                copy.start()
+
+        total = jnp.sum(total, axis=0, keepdims=True)
+        t_begin(0, total)
+        pair_step(0, 0, 0, NB - 1, 0)
+        finish(0)
+
+        def y_all(c):
+            return [
+                remote(
+                    c_send.at[c, lax.rem(dy + rel, 4)],
+                    y_recv.at[c, rel - 1],
+                    sem_ys.at[c, rel - 1],
+                    sem_yr.at[c, rel - 1],
+                    y_peer(rel),
                 )
                 for rel in range(1, 4)
             ]
 
-        def begin_second(c):
-            first = y_first(c)
-            first[0].wait_recv()
-            c_send[c, up, lo2] = c_send[c, up, lo2] + y_a[c, 0]
-            y_second(c)[0].start()
-            first[1].wait_recv()
-            c_send[c, down, hi2] = c_send[c, down, hi2] + y_a[c, 1]
-            y_second(c)[1].start()
+        def z_one(c):
+            return remote(z_send.at[c], z_recv.at[c], sem_zs.at[c], sem_zr.at[c], z_peer(OFFSETS[c]))
+
+        def y_sum(c):
+            value = c_send[c, dy]
+            for k, copy in enumerate(y_all(c)):
+                copy.wait_recv()
+                value = value + y_recv[c, k]
+            return value
 
         def begin_z(c):
-            for copy in y_first(c)[2:] + y_second(c):
-                copy.wait_recv()
-            z_send[c, 0:2] = c_send[c, dy, lo2] + y_b[c, 0] + y_d[c, 1]
-            z_send[c, 2:4] = c_send[c, dy, hi2] + y_b[c, 1] + y_d[c, 0]
-            for copy in z_all(c):
-                copy.start()
-
-        def t_copies(phase):
-            into = t_one if phase == 0 else t_two
-            row = pl.ds(0, 1)
-            peer = dev_peer if phase == 0 else grp_peer
-            return [
-                remote(t_send.at[phase, row], into.at[rel, row], sem_ts.at[phase, rel], sem_tr.at[phase, rel], peer(rel))
-                for rel in range(1, 16)
-            ]
-
-        one, two = t_copies(0), t_copies(1)
-
-        def start(copies):
-            for copy in copies:
-                copy.start()
-
-        total = jnp.sum(total, axis=0, keepdims=True)
-        t_send[0, 0:1] = total
-        start(one)
-        start(y_first(0)[:2])
+            z_send[c] = y_sum(c)
+            z_one(c).start()
+
+        start(y_all(0))
         with jax.named_scope("edges"):
             start_edges()
-        with jax.named_scope("left_loop_1"):
-            lax.fori_loop(0, 1, four_second, 0)
-        start(y_first(0)[2:])
-        with jax.named_scope("left_loop_1"):
-            lax.fori_loop(1, 3, four_second, 0)
-        for pair in (13, 14, 15):
-            pair_step(1, pair, pair % 2, pair * 2 - 1, pair * 2)
-        pair_step(1, 0, 0, NB - 1, 0)
-        finish(1)
-        start(y_first(1)[:2])
-        with jax.named_scope("y_second_0"):
-            begin_second(0)
-        start(y_first(1)[2:])
+        start(y_all(1))
+        with jax.named_scope("left_loop"):
+            lax.fori_loop(0, 4, four_second, 0)
+            finish(1)
+        start(y_all(2))
+        start(y_all(3))
+        with jax.named_scope("z_0"):
+            begin_z(0)
         with jax.named_scope("trace_dev"):
-            for rel in range(1, 16):
-                one[rel - 1].wait_recv()
-                total = total + t_one[rel, 0:1]
-            t_send[1, 0:1] = total
-            start(two)
-        with jax.named_scope("y_second_1"):
-            begin_second(1)
+            total = t_sum(0, total)
+            t_begin(1, total)
         with jax.named_scope("edge_pass"):
             pass_edges()
-        with jax.named_scope("z_0"):
-            begin_z(0)
         with jax.named_scope("z_1"):
             begin_z(1)
+        with jax.named_scope("z_2"):
+            begin_z(2)
+        with jax.named_scope("y_3"):
+            mine = y_sum(3)
         with jax.named_scope("trace_grp"):
-            for rel in range(1, 16):
-                two[rel - 1].wait_recv()
-                total = total + t_two[rel, 0:1]
+            total = t_sum(1, total)
         mean = jnp.sum(total, axis=(0, 1), keepdims=True) * (1.0 / 8192.0)
         scale = jnp.broadcast_to(mean, (32, 2 * T))
 
@@ -507,21 +492,21 @@
                     value = value + jnp.where(match, e_recv[side, 0:32, slot * T : (slot + 1) * T], 0.0)
                 out[:, base + j * T : base + (j + 1) * T] = value / scale[:, :T]
 
-        for c in range(2):
-            value = z_send[c, dz]
-            with jax.named_scope("z_wait"):
-                for k, copy in enumerate(z_all(c)):
-                    copy.wait_recv()
-                    value = value + z_recv[c, k]
-            out[:, 512 + c * 256 : 512 + (c + 1) * 256] = value / scale
+        with jax.named_scope("z_wait"):
+            for c in range(3):
+                z_one(c).wait_recv()
+                mine = mine + z_recv[c]
+        out[:, 512:1024] = mine / jnp.broadcast_to(mean, (32, 4 * T))
 
         done = jax.named_scope("sends_done")
         done.__enter__()
-        for copy in halo_copies + one + two:
+        for copy in halo_copies + t_copies(0) + t_copies(1):
             copy.wait_send()
-        for c in range(2):
-            for copy in y_first(c) + y_second(c) + z_all(c):
+        for c in range(4):
+            for copy in y_all(c):
                 copy.wait_send()
+        for c in range(3):
+            z_one(c).wait_send()
         for side, at in ends:
 
             @pl.when(dev == at)
@@ -539,8 +524,7 @@
     small, other = (
         tuple(tuple(pltpu.ACC(unit)((T, 2 * T), F32) for _ in range(3)) for unit in range(2)) for _ in range(2)
     )
-    large = tuple(pltpu.ACC(unit)((2 * T, 2 * T), F32) for unit in range(2))
-    pl.run_scoped(body, small, other, large)
+    pl.run_scoped(body, small, other)
 
 
 def local(a_tiles, prolong, coarse_ids):
@@ -564,27 +548,24 @@
             vmem((2, 2, T, T), F32),
             vmem((2, 8, 2 * T), jnp.int32),
             vmem((2, 8, 2 * T), jnp.int32),
-            vmem((2, 4, 4, 32, 2 * T), F32),
-            vmem((2, 2, 2, 32, 2 * T), F32),
-            vmem((2, 2, 2, 32, 2 * T), F32),
-            vmem((2, 2, 2, 32, 2 * T), F32),
-            vmem((2, 4, 32, 2 * T), F32),
-            vmem((2, 3, 32, 2 * T), F32),
+            vmem((4, 4, 32, 4 * T), F32),
+            vmem((4, 3, 32, 4 * T), F32),
+            vmem((3, 32, 4 * T), F32),
+            vmem((3, 32, 4 * T), F32),
             vmem((2, 4, 72, 2 * T), F32),
             vmem((2, 72, 2 * T), F32),
             vmem((2, 4, 40, 2 * T), F32),
             vmem((2, 40, 2 * T), F32),
             vmem((2, 8, T), F32),
-            vmem((16, 8, T), F32),
-            vmem((16, 8, T), F32),
+            vmem((2, 16, 8, T), F32),
             dma((8,)),
             dma((8,)),
             dma((4,)),
             dma((4,)),
-            dma((2, 6)),
-            dma((2, 6)),
-            dma((2, 6)),
-            dma((2, 6)),
+            dma((4, 3)),
+            dma((4, 3)),
+            dma((3,)),
+            dma((3,)),
             dma((2, 6)),
             dma((2, 2)),
             dma((2, 16)),

time: 41.3 us -> 39.8 us (0.964)
  the two profiles are of different devices: /device:TPU:39 before, /device:TPU:2 now
where the time goes in v4:
time: 39.8 us; the launch traced here: 39.7 us
  Pallas kernels  38.4 us (96%)
  local copies, waits for them, and re-layouts  1.36 us (3%)
    pallas_call x1, Pallas kernels, local(): pl.pallas_call(kernel, out_shape=jax.ShapeDtypeStruct((32, 1536), F32), i...  38.4 us
    unnamed x3, local copies, waits for them, and re-layouts  1.36 us

profile of v4, /device:TPU:2, one launch (start us, length us, event | category | flops | bytes accessed | tf_op | source)
XLA Modules:
  0.0 39.7 jit_solution(12571112601174721165)
XLA Ops:
  0.0 0.0 copy-start
  0.0 0.7 %copy-done = s32[32,2]{0,1:T(2,128)S(1)} copy-done((s32[32,2]{0,1:T(2,128)S(1)}, s32[32,2]{0,1:T(2,128)}, u32[]{:S(2)}) %copy-start) | copy-done | bytes 280
  0.7 38.4 %shard_map.37 = f32[32,1536]{1,0:T(8,128)S(1)} custom-call(s32[2,32]{1,0:T(2,128)S(1)} %bitcast.2, f32[32,3,128,128]{3,2,1,0:T(8,128)} %a_hbm.1, f32[64,128,128]{2,1,0:T(8,128)} %bitcast.3), custom_call_target="tpu_custom_call" | custom-call | tf_op jit(solution)/shard_map/pallas_call | solution.py:532
  39.0 0.7 %copy.5 = f32[32,1536]{1,0:T(8,128)} copy(f32[32,1536]{1,0:T(8,128)S(1)} %shard_map.37) | data formatting | bytes 393216
Async XLA Ops:
  0.0 0.7 %copy-start = (s32[32,2]{0,1:T(2,128)S(1)}, s32[32,2]{0,1:T(2,128)}, u32[]{:S(2)}) copy-start(s32[32,2]{0,1:T(2,128)} %param.5) | copy-start | bytes 772

commit v5 on v4

--- a/solution.py
+++ b/solution.py
@@ -230,7 +230,7 @@
         with jax.named_scope("right_start"):
             one_group(0)
         with jax.named_scope("right_loop"):
-            lax.fori_loop(0, 1, two_groups, 0)
+            lax.fori_loop(0, 2, two_groups, 0)
         load_p(7).wait()
         with jax.named_scope("barrier"):
             pl.semaphore_wait(barrier, 32)
@@ -243,7 +243,7 @@
         for copy in halo_copies:
             copy.start()
         with jax.named_scope("right_loop"):
-            lax.fori_loop(1, 3, two_groups, 0)
+            lax.fori_loop(2, 3, two_groups, 0)
         with jax.named_scope("right_end"):
             one_group(7)
 

time: 39.8 us -> 39.7 us (level)
  no operation moved by 1% of the time
where the time goes in v5:
time: 39.7 us
  Pallas kernels  38.3 us (96%)
  local copies, waits for them, and re-layouts  1.36 us (3%)
    pallas_call x1, Pallas kernels, local(): pl.pallas_call(kernel, out_shape=jax.ShapeDtypeStruct((32, 1536), F32), i...  38.3 us
    unnamed x3, local copies, waits for them, and re-layouts  1.36 us

profile of v5, /device:TPU:2, one launch (start us, length us, event | category | flops | bytes accessed | tf_op | source)
XLA Modules:
  0.0 39.7 jit_solution(997611584431301741)
XLA Ops:
  0.0 0.0 copy-start
  0.0 0.7 %copy-done = s32[32,2]{0,1:T(2,128)S(1)} copy-done((s32[32,2]{0,1:T(2,128)S(1)}, s32[32,2]{0,1:T(2,128)}, u32[]{:S(2)}) %copy-start) | copy-done | bytes 280
  0.7 38.3 %shard_map.37 = f32[32,1536]{1,0:T(8,128)S(1)} custom-call(s32[2,32]{1,0:T(2,128)S(1)} %bitcast.2, f32[32,3,128,128]{3,2,1,0:T(8,128)} %a_hbm.1, f32[64,128,128]{2,1,0:T(8,128)} %bitcast.3), custom_call_target="tpu_custom_call" | custom-call | tf_op jit(solution)/shard_map/pallas_call | solution.py:532
  39.0 0.7 %copy.5 = f32[32,1536]{1,0:T(8,128)} copy(f32[32,1536]{1,0:T(8,128)S(1)} %shard_map.37) | data formatting | bytes 393216
Async XLA Ops:
  0.0 0.7 %copy-start = (s32[32,2]{0,1:T(2,128)S(1)}, s32[32,2]{0,1:T(2,128)}, u32[]{:S(2)}) copy-start(s32[32,2]{0,1:T(2,128)} %param.5) | copy-start | bytes 772
